TPU v7x, 32 devices: a whole 2x2x4 slice. The times are simulated.
32 devices in a mesh: dp: 2 (over x), ep: 16 (over z, y, core).
Axes of the slice: x: 2, y: 2, z: 4, core: 2. Of those that a mesh axis runs over, the one named last changes fastest.
Arguments:
- tokens: bfloat16 [262144, 768], P(('dp', 'ep')), parts along dimension 0
- expert_idx: int32 [262144], P(('dp', 'ep')), parts along dimension 0
- w_router: float32 [768, 32], replicated
- w_in: bfloat16 [32, 768, 3072], P('ep')
- w_out: bfloat16 [32, 3072, 768], P('ep')
Outputs:
- output: bfloat16 [262144, 768], P(('dp', 'ep')), parts along dimension 0
There are 2 independent parts. A program takes and returns all parts, laid end to end along the dimension named above; an argument that names none is the same for every part.
All inputs are finite; a program needn't handle non-finite values.
Results may differ from a plain program's by a relative error of at most 0.001.
Values are sent between devices in bfloat16 or wider.
A program may use at most 1 GiB of HBM per device.

v0:
```python
import jax
import jax.numpy as jnp
from jax import lax
from jax.sharding import PartitionSpec as P, NamedSharding


def dispatch(tok_rows, choice, w_router, capacity):
    tok_count = tok_rows.shape[0]
    num_experts = w_router.shape[1]
    logits = jnp.dot(tok_rows.astype(jnp.float32), w_router, precision=lax.Precision.HIGHEST)
    router_prob = jax.nn.softmax(logits, axis=-1)
    chosen = choice[:, None] == jnp.arange(num_experts, dtype=jnp.int32)[None, :]
    gate_prob = jnp.sum(jnp.where(chosen, router_prob, 0.0), axis=-1)
    running_count = jnp.cumsum(chosen.astype(jnp.int32), axis=0) - 1
    position = jnp.sum(jnp.where(chosen, running_count, 0), axis=-1)
    slot_index = jnp.where(position < capacity, choice * capacity + position, num_experts * capacity)
    holder = jnp.full((num_experts * capacity + 1,), tok_count, jnp.int32).at[slot_index].set(jnp.arange(tok_count, dtype=jnp.int32))
    buffer = jnp.take(tok_rows, holder[:-1], axis=0, mode="fill", fill_value=0)
    return buffer, slot_index, gate_prob


def combine(flat_out, slot_index, gate_prob):
    picked = jnp.take(flat_out, slot_index, axis=0, mode="fill", fill_value=0)
    return (gate_prob[:, None] * picked.astype(jnp.float32)).astype(jnp.bfloat16)


def solution(mesh):
    groups = mesh.shape["ep"]

    def local_block(tokens, expert_idx, w_router, w_in, w_out):
        tok_count, model_dim = tokens.shape
        local_experts = w_in.shape[0]
        num_experts = local_experts * groups
        capacity = (5 * tok_count + 4 * num_experts - 1) // (4 * num_experts)
        buffer, slot_index, gate_prob = dispatch(tokens, expert_idx, w_router, capacity)
        send_buf = buffer.reshape(groups, local_experts, capacity, model_dim)
        recv_buf = lax.all_to_all(send_buf, "ep", 0, 2, tiled=True)
        rows_in = recv_buf.reshape(local_experts, groups * capacity, model_dim)
        hidden = jnp.einsum("ecd,edf->ecf", rows_in, w_in, preferred_element_type=jnp.float32)
        hidden_act = jax.nn.relu(hidden).astype(jnp.bfloat16)
        expert_rows = jnp.einsum("ecf,efd->ecd", hidden_act, w_out, preferred_element_type=jnp.float32).astype(jnp.bfloat16)
        back_buf = lax.all_to_all(expert_rows.reshape(1, local_experts, groups * capacity, model_dim), "ep", 2, 0, tiled=True)
        flat_out = back_buf.reshape(num_experts * capacity, model_dim)
        return combine(flat_out, slot_index, gate_prob)

    return jax.shard_map(local_block, mesh=mesh, in_specs=(P(("dp", "ep"), None), P(("dp", "ep")), P(None, None), P("ep", None, None), P("ep", None, None)), out_specs=P(("dp", "ep"), None), check_vma=False)
```

profile of v0, /device:TPU:13, one launch (start us, length us, event | category | flops | bytes accessed | tf_op | source)
XLA Modules:
  0.0 1022.2 jit_solution(1657437447254206386)
XLA Ops:
  0.0 0.0 copy-start
  0.0 0.9 fusion.4
  0.9 9.5 reduce-window.6
  10.4 0.9 slice_reduce_fusion
  11.4 0.2 reduce-window.9
  11.6 0.3 add_add_fusion
  11.9 1.5 fusion.3
  13.4 0.0 copy-start.2
  13.4 0.6 copy-done.2
  14.0 1.4 fusion.7
  15.4 30.5 %scatter_custom_fusion = s32[10241]{0:T(1024)S(1)} fusion(s32[8192]{0:T(1024)S(1)} %get-tuple-element.6, s32[8192]{0:T(1024)S(1)} %iota.11, s32[]{:T(128)} %constant.31.clone.1), kind=kCustom, calls=%fused_computation.29 | custom fusion | bytes 40968 | tf_op jit(solution)/shard_map/scatter | solution.py:17
  45.9 0.1 slice.14
  46.0 0.1 compare_and_fusion
  46.1 52.3 %gather_fusion = bf16[10240,768]{1,0:T(8,128)(2,1)} fusion(bf16[8192,768]{1,0:T(8,128)(2,1)} %param.5, s32[10240]{0:T(1024)S(1)} %get-tuple-element.8), kind=kCustom, calls=%fused_computation | custom fusion | bytes 31498240 | tf_op jit(solution)/shard_map/jit(_take)/gather | solution.py:18
  98.4 8.2 broadcast_select_fusion
  106.6 346.3 %all_to_all.30 = bf16[16,2,320,768]{3,2,1,0:T(8,128)(2,1)S(1)} all-to-all(bf16[16,2,320,768]{3,2,1,0:T(8,128)(2,1)S(1)} %broadcast_select_fusion), channel_id=1, replica_groups=mesh['dp'=2,'ep'=16] {'ep'}, dimensions={0} | all-to-all | bytes 31457280 | tf_op jit(solution)/shard_map/all_to_all | solution.py:37
  452.8 6.3 copy.12
  459.2 58.5 %fusion.13 = bf16[2,5120,3072]{2,1,0:T(8,128)(2,1)} fusion(bf16[2,5120,768]{2,1,0:T(8,128)(2,1)} %bitcast.36, bf16[2,768,3072]{2,1,0:T(8,128)(2,1)} %param.8), kind=kOutput, calls=%fused_computation.34 | convolution fusion | flops 48318382080 | bytes 88080384 | tf_op jit(solution)/shard_map/ecd,edf->ecf/dot_general | solution.py:39
  517.7 57.4 %convert_bitcast_fusion = bf16[1,2,5120,768]{3,2,1,0:T(8,128)(2,1)} fusion(bf16[2,3072,768]{2,1,0:T(8,128)(2,1)} %param.9, bf16[2,5120,3072]{2,1,0:T(8,128)(2,1)} %fusion.13), kind=kOutput, calls=%fused_computation.7 | convolution fusion | flops 48420618240 | bytes 88080384 | tf_op jit(solution)/shard_map/ecf,efd->ecd/dot_general | solution.py:41
  575.1 29.6 %copy.13 = bf16[1,2,5120,768]{3,1,0,2:T(2,128)(2,1)} copy(bf16[1,2,5120,768]{3,2,1,0:T(8,128)(2,1)} %convert_bitcast_fusion) | data formatting | bytes 31457280 | tf_op jit(solution)/shard_map/reshape | solution.py:42
  604.7 5.1 all-to-all-start.1
  609.8 0.0 copy-done
  609.8 0.0 copy-start.1
  609.8 0.0 copy-start.3
  609.8 13.8 %fusion.12 = (f32[8192]{0:T(1024)S(1)}, f32[8192,32]{0,1:T(8,128)S(1)}) fusion(bf16[8192,768]{1,0:T(8,128)(2,1)} %param.5, f32[768,32]{0,1:T(8,128)S(1)} %copy-done), kind=kOutput, calls=%fused_computation.33 | convolution fusion | flops 2416173056 | bytes 13762560 | tf_op jit(solution)/shard_map/dot_general | solution.py:10
  623.6 0.2 fusion.5
  623.8 0.0 copy-done.1
  623.8 0.0 copy-done.3
  623.9 0.3 select_reduce_fusion
  624.2 325.7 %all-to-all-done.1 = bf16[1,2,5120,768]{3,1,0,2:T(2,128)(2,1)} async-done(((bf16[1,2,5120,768]{3,1,0,2:T(2,128)(2,1)}), bf16[1,2,5120,768]{3,1,0,2:T(2,128)(2,1)}, u32[]{:S(2)}, u32[]{:S(2)}) %all-to-all-start.1) | async-done | bytes 15728672 | tf_op jit(solution)/shard_map/all_to_all | solution.py:42
  949.8 0.0 copy-start.4
  949.8 15.2 %copy.14 = bf16[1,2,16,320,768]{4,3,1,2,0:T(8,128)(2,1)} copy(bf16[1,2,16,320,768]{4,1,3,2,0:T(2,128)(2,1)} %bitcast.7) | data formatting | bytes 31457280 | tf_op jit(solution)/shard_map/all_to_all | solution.py:42
  965.0 0.0 copy-done.4
  965.0 44.5 %gather_fusion.1 = bf16[8192,768]{1,0:T(8,128)(2,1)} fusion(bf16[10240,768]{1,0:T(8,128)(2,1)} %bitcast.34, s32[8192]{0:T(1024)S(1)} %copy-done.4), kind=kCustom, calls=%fused_computation.1 | custom fusion | bytes 25198592 | tf_op jit(solution)/shard_map/jit(_take)/gather | solution.py:23
  1009.6 12.7 %multiply_convert_fusion = bf16[8192,768]{1,0:T(8,128)(2,1)} fusion(bf16[8192,768]{1,0:T(8,128)(2,1)} %gather_fusion.1, f32[8192]{0:T(1024)S(1)} %select_reduce_fusion, pred[8192]{0:T(1024)(128)(4,1)S(1)} %compare_and_fusion.1), kind=kLoop, calls=%fused_computation.6 | loop fusion | flops 25165824 | bytes 25206784 | tf_op jit(solution)/shard_map/convert_element_type | solution.py:24
  (3 shorter events, 0.0 us)
Async XLA Ops:
  0.0 609.8 %copy-start = (f32[768,32]{0,1:T(8,128)S(1)}, f32[768,32]{0,1:T(8,128)}, u32[]{:S(2)}) copy-start(f32[768,32]{0,1:T(8,128)} %param.7) | copy-start | bytes 294916
  13.4 0.6 copy-start.2
  604.7 345.1 %all-to-all-start.1 = ((bf16[1,2,5120,768]{3,1,0,2:T(2,128)(2,1)}), bf16[1,2,5120,768]{3,1,0,2:T(2,128)(2,1)}, u32[]{:S(2)}, u32[]{:S(2)}) async-start(bf16[1,2,5120,768]{3,1,0,2:T(2,128)(2,1)} %copy.13), calls=%async_computation.1 | async-start | bytes 31457280 | tf_op jit(solution)/shard_map/all_to_all | solution.py:42
  609.8 14.0 %copy-start.1 = (s32[8192]{0:T(1024)S(1)}, s32[8192]{0:T(1024)}, u32[]{:S(2)}) copy-start(s32[8192]{0:T(1024)} %param.6) | copy-start | bytes 98308
  609.8 14.0 %copy-start.3 = (s32[8192]{0:T(1024)S(1)}, s32[8192]{0:T(1024)}, u32[]{:S(2)}) copy-start(s32[8192]{0:T(1024)} %copy-done.2) | copy-start | bytes 98308
  949.8 15.2 %copy-start.4 = (s32[8192]{0:T(1024)S(1)}, s32[8192]{0:T(1024)}, u32[]{:S(2)}) copy-start(s32[8192]{0:T(1024)} %get-tuple-element.5) | copy-start | bytes 98308
where the time goes:
time: 1020 us
  blocking collectives  346 us (34%)
  waiting for transfers between devices  326 us (32%)
  local copies, waits for them, and re-layouts  180 us (18%)
  matrix products  130 us (13%)
  other arithmetic  35.3 us (3%)
    all_to_all x1, blocking collectives, local_block(): recv_buf = lax.all_to_all(send_buf, 'ep', 0, 2, tiled=True)  346 us
    all_to_all x1, waiting for transfers between devices, local_block(): lax.all_to_all(expert_rows.reshape(1, local_experts, groups * capacity, m...  326 us
    dot_general x1, matrix products, local_block(): jnp.einsum('ecd,edf->ecf', rows_in, w_in, preferred_element_type=jnp.floa...  58.5 us
    dot_general x1, matrix products, local_block(): jnp.einsum('ecf,efd->ecd', hidden_act, w_out, preferred_element_type=jnp....  57.4 us
    gather x1, local copies, waits for them, and re-layouts, dispatch(): buffer = jnp.take(tok_rows, holder[:-1], axis=0, mode='fill', fill_value=0)  52.3 us
    gather x1, local copies, waits for them, and re-layouts, combine(): picked = jnp.take(flat_out, slot_index, axis=0, mode='fill', fill_value=0)  44.5 us
    scatter x1, local copies, waits for them, and re-layouts, dispatch(): jnp.full((num_experts * capacity + 1,), tok_count, jnp.int32).at[slot_index]  30.5 us
    reshape x1, local copies, waits for them, and re-layouts, local_block(): expert_rows.reshape(1, local_experts, groups * capacity, model_dim)  29.6 us
  transfers between devices with their start and end apart: 1, of which 1 were waited for; matrix products, arithmetic and copies ran while one was open for 1% of the time, Pallas kernels for 0%

commit v1 on v0

v1 whole, which is shorter than its diff:
```python
import jax
import jax.numpy as jnp
from jax import lax
from jax.experimental import pallas as pl
from jax.experimental.pallas import tpu as pltpu
from jax.sharding import PartitionSpec as P

AXES = ("dp", "ep")
MESH = pl.DeviceIdType.MESH
PAIRS = 4


def exchange_body(disp, w_in, w_out, wb_in, wc_in,
                  back, wb_out, wc_out, wd_in, wd_out,
                  xs, wi, wo, hid, x_send, x_recv, w_send, w_recv, r_send, b_recv, w_load):
    x = lax.axis_index("dp")
    ep = lax.axis_index("ep")
    z, y, c = ep // 4, (ep // 2) % 2, ep % 2
    inner = (z == 1) | (z == 2)
    z_near = z + 1 - 2 * (z % 2)
    z_mid = 3 - z

    def device(m, slab):
        return ((x + m // 4) % 2, slab * 4 + ((y + (m // 2) % 2) % 2) * 2 + (c + m % 2) % 2)

    def remote(src, dst, send, recv, dev):
        return pltpu.make_async_remote_copy(src, dst, send, recv, device_id=dev, device_id_type=MESH)

    barrier = pltpu.get_barrier_semaphore()
    for m in range(1, 8):
        pl.semaphore_signal(barrier, inc=1, device_id=device(m, z), device_id_type=MESH)
    for m in range(8):
        pl.semaphore_signal(barrier, inc=1, device_id=device(m, z_near), device_id_type=MESH)
    pl.semaphore_signal(barrier, inc=1, device_id=device(0, z_mid), device_id_type=MESH)
    pl.semaphore_wait(barrier, 16)

    send_b = remote(w_out.at[x], wb_out, w_send.at[0], w_recv.at[0], device(0, z_near))
    send_c = remote(w_out.at[x], wc_out, w_send.at[1], w_recv.at[1], device(0, z_mid))
    send_di = remote(wb_in, wd_in, w_send.at[2], w_recv.at[2], device(0, z_mid))
    send_do = remote(wb_out, wd_out, w_send.at[3], w_recv.at[3], device(0, z_mid))

    def load(src, dst, k):
        return pltpu.make_async_copy(src, dst, w_load.at[k])

    load_a = (load(w_in.at[x], wi.at[0], 0), load(w_out.at[x], wo.at[0], 1))
    load_b = (load(wb_in, wi.at[1], 2), load(wb_out, wo.at[1], 3))
    load_c = (load(wc_in, wi.at[0], 0), load(wc_out, wo.at[0], 1))
    load_d = (load(wd_in, wi.at[1], 2), load(wd_out, wo.at[1], 3))

    send_b.start()

    @pl.when(inner)
    def _():
        send_c.start()
        send_di.start()

    def own(q, r):
        return pltpu.make_async_copy(disp.at[q, 0], xs.at[r, 0], x_recv.at[r, 0])

    def dispatch(q, r, m, slab):
        return remote(disp.at[q, m], xs.at[r, m], x_send.at[q, m], x_recv.at[r, m], device(m, slab))

    for copy in load_a:
        copy.start()
    load_b[0].start()
    own(0, 0).start()
    own(1, 1).start()

    order = (1, 2, 4, 3, 5, 6, 7)
    for m in order:
        dispatch(0, 0, m, z).start()
    for m in order:
        dispatch(1, 1, m, z).start()

    @pl.when(inner)
    def _():
        own(2, 2).start()
        own(3, 5).start()
        for m in order:
            dispatch(2, 2, m, z).start()
        for m in order:
            dispatch(3, 5, m, z).start()

    @pl.when(jnp.logical_not(inner))
    def _():
        for m in range(8):
            dispatch(2, 3, m, z_near).start()
        for m in range(8):
            dispatch(3, 4, m, z_near).start()

    cap, dim = xs.shape[2:]
    hidden = wi.shape[2]
    rows = 2 * cap
    tile_in, tile_out = 512, 256

    def compute(r, p, b):
        view = xs.at[r]

        def first(n, carry):
            cols = pl.ds(pl.multiple_of(n * tile_in, tile_in), tile_in)
            value = jnp.dot(view[pl.ds(2 * p, 2)].reshape(rows, dim), wi[b, :, cols], preferred_element_type=jnp.float32)
            hid[:, cols] = jnp.maximum(value, 0.0).astype(jnp.bfloat16)
            return carry

        lax.fori_loop(0, hidden // tile_in, first, 0)

        def second(n, carry):
            cols = pl.ds(pl.multiple_of(n * tile_out, tile_out), tile_out)
            value = jnp.dot(hid[...], wo[b, :, cols], preferred_element_type=jnp.float32)
            view[pl.ds(2 * p, 2), :, cols] = value.astype(jnp.bfloat16).reshape(2, cap, tile_out)
            return carry

        lax.fori_loop(0, dim // tile_out, second, 0)

    def landed(sem):
        pltpu.make_async_copy(xs.at[0, 0], xs.at[0, 0], sem).wait()

    def job(j, carry):
        r, p = j // PAIRS, j % PAIRS

        @pl.when(j == 0)
        def _():
            load_a[0].wait()
            load_a[1].wait()

        @pl.when(j == PAIRS)
        def _():
            send_b.wait_recv()
            load_b[1].start()

            @pl.when(inner)
            def _():
                send_do.start()
                load_c[0].start()

            load_b[0].wait()
            load_b[1].wait()

        @pl.when(j == 2 * PAIRS)
        def _():
            send_c.wait_recv()
            load_c[1].start()
            load_c[0].wait()
            load_c[1].wait()

        @pl.when(j == 4 * PAIRS)
        def _():
            send_di.wait_recv()
            load_d[0].start()
            send_do.wait_recv()
            load_d[1].start()
            load_d[0].wait()
            load_d[1].wait()

        landed(x_recv.at[r, 2 * p])
        landed(x_recv.at[r, 2 * p + 1])
        late = r // 4
        kind = jnp.where(r == 1, 1, late)
        compute(r, p, kind)
        edge = (r == 3) | (r == 4)
        q = jnp.where(r < 2, 0, 2) + kind
        slab = jnp.where(edge, z_near, z)

        def result(m):
            return remote(xs.at[r, m], back.at[q, m], r_send.at[r, m], b_recv.at[q, m], device(m, slab))

        keep = (p == 0) & jnp.logical_not(edge)

        @pl.when(keep)
        def _():
            pltpu.make_async_copy(xs.at[r, 0], back.at[q, 0], b_recv.at[q, 0]).start()

        @pl.when(jnp.logical_not(keep))
        def _():
            result(2 * p).start()

        result(2 * p + 1).start()
        return carry

    lax.fori_loop(0, jnp.where(inner, 6 * PAIRS, 2 * PAIRS), job, 0)

    def each(fn, lo, hi):
        def step(i, carry):
            fn(i)
            return carry

        lax.fori_loop(lo, hi, step, 0)

    skip = jnp.where(inner, 1, 0)
    for q in range(4):
        each(lambda m: landed(b_recv.at[q, m]), 0, 8)
        each(lambda m: landed(x_send.at[q, m]), 1 if q < 2 else skip, 8)
    for r in (0, 1):
        each(lambda m: landed(r_send.at[r, m]), 1, 8)
    send_b.wait_send()

    @pl.when(inner)
    def _():
        for r in (2, 3, 4, 5):
            each(lambda m: landed(r_send.at[r, m]), 0 if r in (3, 4) else 1, 8)
        send_c.wait_send()
        send_di.wait_send()
        send_do.wait_send()


def exchange(disp, w_in, w_out, wb_in, wc_in):
    _, _, cap, dim = disp.shape
    hidden = w_in.shape[2]
    anywhere = pl.BlockSpec(memory_space=pl.ANY)
    dma = pltpu.SemaphoreType.DMA
    bf16 = jnp.bfloat16
    in_shape, out_shape = (dim, hidden), (hidden, dim)
    outs = [disp.shape, out_shape, out_shape, in_shape, out_shape]
    return pl.pallas_call(
        exchange_body,
        in_specs=[anywhere] * 5,
        out_specs=[anywhere] * 5,
        out_shape=[jax.ShapeDtypeStruct(s, bf16) for s in outs],
        scratch_shapes=[
            pltpu.VMEM((6, 8, cap, dim), bf16),
            pltpu.VMEM((2,) + in_shape, bf16),
            pltpu.VMEM((2,) + out_shape, bf16),
            pltpu.VMEM((2 * cap, hidden), bf16),
            dma((4, 8)), dma((6, 8)), dma((4,)), dma((4,)), dma((6, 8)), dma((4, 8)), dma((4,)),
        ],
        compiler_params=pltpu.CompilerParams(collective_id=0, has_side_effects=True, vmem_limit_bytes=60 << 20),
        cost_estimate=pl.CostEstimate(flops=4 * 48 * cap * dim * hidden, bytes_accessed=100 << 20, transcendentals=0),
        name="exchange",
    )(disp, w_in, w_out, wb_in, wc_in)[0]


def lin(x, z, y, c):
    return x * 16 + z * 4 + y * 2 + c


DEVICES = [(x, z, y, c) for x in range(2) for z in range(4) for y in range(2) for c in range(2)]


def solution(mesh):
    swap_near = [(lin(x, z, y, c), lin(x, z ^ 1, y, c)) for x, z, y, c in DEVICES]
    swap_mid = [(lin(x, z, y, c), lin(x, 3 - z, y, c)) for x, z, y, c in DEVICES if z in (1, 2)]

    def local_block(tokens, expert_idx, w_router, w_in, w_out):
        tok_count, dim = tokens.shape
        num_experts = w_router.shape[1]
        capacity = (5 * tok_count + 4 * num_experts - 1) // (4 * num_experts)
        x = lax.axis_index("dp")
        ep = lax.axis_index("ep")
        z, y, c = ep // 4, (ep // 2) % 2, ep % 2

        wa_in = lax.dynamic_index_in_dim(w_in, x, 0, False)
        with jax.named_scope("weights_mid"):
            wc_in = lax.ppermute(wa_in, AXES, swap_mid)
        with jax.named_scope("weights_near"):
            wb_in = lax.ppermute(wa_in, AXES, swap_near)

        logits = jnp.dot(tokens.astype(jnp.float32), w_router, precision=lax.Precision.HIGHEST)
        router_prob = jax.nn.softmax(logits, axis=-1)
        chosen = expert_idx[:, None] == jnp.arange(num_experts, dtype=jnp.int32)[None, :]
        gate = jnp.sum(jnp.where(chosen, router_prob, 0.0), axis=-1)
        running = jnp.cumsum(chosen.astype(jnp.int32), axis=0) - 1
        position = jnp.sum(jnp.where(chosen, running, 0), axis=-1)

        bit_x, bit_c, bit_y, slab = expert_idx & 1, (expert_idx >> 1) & 1, (expert_idx >> 2) & 1, expert_idx >> 3
        mask = ((bit_x ^ x) << 2) | ((bit_y ^ y) << 1) | (bit_c ^ c)
        far = (slab >> 1) != (z >> 1)
        second = jnp.where(far, (slab == 0) | (slab == 3), slab != z)
        block = far.astype(jnp.int32) * 16 + second.astype(jnp.int32) * 8 + mask
        kept = position < capacity
        slot = jnp.where(kept, block * capacity + position, num_experts * capacity)
        holder = jnp.zeros((num_experts * capacity + 1,), jnp.int32).at[slot].set(jnp.arange(tok_count, dtype=jnp.int32))
        disp = jnp.take(tokens, holder[:-1], axis=0, mode="clip").reshape(4, 8, capacity, dim)

        back = exchange(disp, w_in, w_out, wb_in, wc_in)

        picked = jnp.take(back.reshape(num_experts * capacity, dim), jnp.where(kept, slot, 0), axis=0, mode="clip")
        scaled = (gate[:, None] * picked.astype(jnp.float32)).astype(jnp.bfloat16)
        return jnp.where(kept[:, None], scaled, jnp.zeros_like(scaled))

    return jax.shard_map(local_block, mesh=mesh, in_specs=(P(AXES, None), P(AXES), P(None, None), P("ep", None, None), P("ep", None, None)), out_specs=P(AXES, None), check_vma=False)
```

time: 1020 us -> 614 us (0.60)
  Pallas kernels: 0 us -> 432 us
  blocking collectives: 346 us -> 0 us
  waiting for transfers between devices: 326 us -> 0.01 us
  matrix products: 130 us -> 13.8 us
  local copies, waits for them, and re-layouts: 180 us -> 133 us
    pallas_call x0 -> x1, Pallas kernels: none -> 432 us  [exchange(): pl.pallas_call(exchange_body, in_specs=[anywhere] * 5, out_specs=[anywher...]
    all_to_all x1 -> x0, blocking collectives: 346 us -> none  [local_block(): recv_buf = lax.all_to_all(send_buf, 'ep', 0, 2, tiled=True)]
    all_to_all x1 -> x0, waiting for transfers between devices: 326 us -> none  [local_block(): lax.all_to_all(expert_rows.reshape(1, local_experts, groups * capacity, m...]
    dot_general x3 -> x1, matrix products: 130 us -> 13.8 us  [local_block(): jnp.dot(tokens.astype(jnp.float32), w_router, precision=lax.Precision.HIG...]
    reshape x1 -> x0, local copies, waits for them, and re-layouts: 29.6 us -> none  [local_block(): expert_rows.reshape(1, local_experts, groups * capacity, model_dim)]
    all_to_all x2 -> x0, local copies, waits for them, and re-layouts: 21.5 us -> none  [the longest x1 15.2 us: local_block(): lax.all_to_all(expert_rows.reshape(1, local_experts, groups * capacity, m...]
    convert_element_type x2 -> x1, other arithmetic: 13.6 us -> 0.87 us  [local_block(): running = jnp.cumsum(chosen.astype(jnp.int32), axis=0) - 1]
  transfers between devices with their start and end apart: 1 -> 2, of which waited for: 1 -> 0; matrix products, arithmetic and copies ran while one was open for 1% -> 18% of each run, Pallas kernels for 0% -> 0%
where the time goes in v1:
time: 614 us; the launch traced here: 610 us
  Pallas kernels  432 us (70%)
  local copies, waits for them, and re-layouts  133 us (22%)
  other arithmetic  26.2 us (4%)
  matrix products  13.8 us (2%)
    pallas_call x1, Pallas kernels, exchange(): pl.pallas_call(exchange_body, in_specs=[anywhere] * 5, out_specs=[anywher...  432 us
    gather x1, local copies, waits for them, and re-layouts, local_block(): jnp.take(tokens, holder[:-1], axis=0, mode='clip')  52.3 us
    gather x1, local copies, waits for them, and re-layouts, local_block(): jnp.take(back.reshape(num_experts * capacity, dim), jnp.where(kept, slot,...  44.5 us
    scatter x1, local copies, waits for them, and re-layouts, local_block(): jnp.zeros((num_experts * capacity + 1,), jnp.int32).at[slot]  30.5 us
    dot_general x1, matrix products, local_block(): jnp.dot(tokens.astype(jnp.float32), w_router, precision=lax.Precision.HIG...  13.8 us
    select_n x1, other arithmetic, local_block(): return jnp.where(kept[:, None], scaled, jnp.zeros_like(scaled))  12.7 us
  transfers between devices with their start and end apart: 2, of which 0 were waited for; matrix products, arithmetic and copies ran while one was open for 18% of the time, Pallas kernels for 0%

profile of v1, /device:TPU:13, one launch (start us, length us, event | category | flops | bytes accessed | tf_op | source)
XLA Modules:
  0.0 610.1 jit_solution(8008598330072129474)
XLA Ops:
  0.0 0.0 copy-start
  0.0 0.0 copy-start.2
  0.0 4.9 dynamic-slice_bitcast_fusion
  4.9 0.2 collective-permute-start
  5.1 4.3 collective-permute-start.1
  9.4 0.9 fusion.3
  10.3 9.5 %reduce-window.6 = s32[32,64,128]{2,1,0:T(8,128)S(1)} reduce-window(s32[32,64,128]{2,1,0:T(8,128)S(1)} %fusion.3, s32[]{:T(128)} %constant.66.clone.1), window={size=1x1x128 pad=0_0x0_0x127_0}, to_apply=%region_0.1 | reduce-window | flops 33292288 | bytes 2097156 | tf_op jit(solution)/shard_map/reduce-window
  19.8 0.9 slice_reduce_fusion
  20.8 0.2 reduce-window.9
  21.0 0.3 add_add_fusion
  21.3 0.0 copy-done.2
  21.3 0.8 fusion.2
  22.1 0.7 select_clamp_fusion
  22.8 30.5 %scatter_custom_fusion = s32[10241]{0:T(1024)S(1)} fusion(s32[8192]{0:T(1024)S(1)} %compare_select_fusion, s32[8192]{0:T(1024)S(1)} %iota.11, s32[]{:T(128)} %constant.66.clone.1), kind=kCustom, calls=%fused_computation.25 | custom fusion | bytes 40968 | tf_op jit(solution)/shard_map/scatter | solution.py:271
  53.3 52.3 %gather_fusion = bf16[10240,768]{1,0:T(8,128)(2,1)} fusion(bf16[8192,768]{1,0:T(8,128)(2,1)} %param.5, s32[10240]{0:T(1024)S(1)} %slice_clamp_fusion), kind=kCustom, calls=%fused_computation | custom fusion | bytes 31498240 | tf_op jit(solution)/shard_map/jit(_take)/gather | solution.py:272
  105.6 0.0 copy-done
  105.6 13.8 %fusion.8 = (f32[8192]{0:T(1024)S(1)}, f32[8192,32]{0,1:T(8,128)S(1)}) fusion(bf16[8192,768]{1,0:T(8,128)(2,1)} %param.5, f32[768,32]{0,1:T(8,128)S(1)} %copy-done), kind=kOutput, calls=%fused_computation.28 | convolution fusion | flops 2416173056 | bytes 13762560 | tf_op jit(solution)/shard_map/dot_general | solution.py:257
  119.4 0.2 fusion.4
  119.6 0.9 select_reduce_fusion
  120.5 0.0 collective-permute-done.wb_in
  120.5 0.0 collective-permute-done.1.wc_in
  120.5 0.0 copy-start.4
  120.5 432.3 %exchange.1 = (bf16[4,8,320,768]{3,2,1,0:T(8,128)(2,1)}, bf16[3072,768]{1,0:T(8,128)(2,1)}, bf16[3072,768]{1,0:T(8,128)(2,1)}, bf16[768,3072]{1,0:T(8,128)(2,1)}, bf16[3072,768]{1,0:T(8,128)(2,1)}) custom-call(bf16[4,8,320,768]{3,2,1,0:T(8,128)(2,1)} %bitcast.22, bf16[2,768,3072]{2,1,0:T(8,128)(2,1)} %w_in.1, bf16[2,3072,768]{2,1,0:T(8,128)(2,1)} %w_out.1, ...), custom_call_target="tpu_custom_call" | custom-call | flops 144955146240 | bytes 104857600 | tf_op jit(solution)/shard_map/exchange/pallas_call | solution.py:214
  552.8 0.0 copy-done.4
  552.8 0.0 copy-start.3
  552.8 0.0 copy-start.5
  552.8 44.5 %gather_fusion.1 = bf16[8192,768]{1,0:T(8,128)(2,1)} fusion(bf16[10240,768]{1,0:T(8,128)(2,1)} %bitcast.21, s32[8192]{0:T(1024)S(1)} %copy-done.4), kind=kCustom, calls=%fused_computation.1 | custom fusion | bytes 25198592 | tf_op jit(solution)/shard_map/jit(_take)/gather | solution.py:276
  597.4 0.0 copy-start.1
  597.4 0.0 copy-done.3
  597.4 0.0 copy-done.5
  597.4 12.7 %fusion = bf16[8192,768]{1,0:T(8,128)(2,1)} fusion(bf16[8192,768]{1,0:T(8,128)(2,1)} %gather_fusion.1, f32[8192]{0:T(1024)S(1)} %copy-done.3, pred[8192]{0:T(1024)(128)(4,1)S(1)} %copy-done.5), kind=kLoop, calls=%fused_computation.4 | loop fusion | flops 25165824 | bytes 25206784 | tf_op jit(solution)/shard_map/jit(_where)/select_n | solution.py:278
  610.1 0.0 copy-done.1
  (3 shorter events, 0.0 us)
Async XLA Ops:
  0.0 105.6 %copy-start = (f32[768,32]{0,1:T(8,128)S(1)}, f32[768,32]{0,1:T(8,128)}, u32[]{:S(2)}) copy-start(f32[768,32]{0,1:T(8,128)} %param.7) | copy-start | bytes 294916
  0.0 21.3 %copy-start.2 = (s32[8192]{0:T(1024)S(1)}, s32[8192]{0:T(1024)}, u32[]{:S(2)}) copy-start(s32[8192]{0:T(1024)} %param.6) | copy-start | bytes 98308
  4.9 115.6 %collective-permute-start = (bf16[768,3072]{1,0:T(8,128)(2,1)}, bf16[768,3072]{1,0:T(8,128)(2,1)}, u32[]{:S(2)}, u32[]{:S(2)}) collective-permute-start(bf16[768,3072]{1,0:T(8,128)(2,1)} %dynamic-slice_bitcast_fusion), channel_id=1, source_target_pairs={{0,4},{1,5},{2,6},{3,7},{4,0},{5,1},{6,2},{7,3},{8,12},{9,13},{10,... | collective-permute-start | bytes 14155784 | tf_op jit(solution)/shard_map/weights_near/ppermute | solution.py:255
  5.1 115.4 %collective-permute-start.1 = (bf16[768,3072]{1,0:T(8,128)(2,1)}, bf16[768,3072]{1,0:T(8,128)(2,1)}, u32[]{:S(2)}, u32[]{:S(2)}) collective-permute-start(bf16[768,3072]{1,0:T(8,128)(2,1)} %dynamic-slice_bitcast_fusion), channel_id=1, source_target_pairs={{4,8},{5,9},{6,10},{7,11},{8,4},{9,5},{10,6},{11,7},{20,24},{21,25... | collective-permute-start | bytes 14155784 | tf_op jit(solution)/shard_map/weights_mid/ppermute | solution.py:253
  120.5 432.3 %copy-start.4 = (s32[8192]{0:T(1024)S(1)}, s32[8192]{0:T(1024)}, u32[]{:S(2)}) copy-start(s32[8192]{0:T(1024)} %get-tuple-element.7) | copy-start | bytes 98308
  552.8 44.6 %copy-start.3 = (f32[8192]{0:T(1024)S(1)}, f32[8192]{0:T(1024)}, u32[]{:S(2)}) copy-start(f32[8192]{0:T(1024)} %select_reduce_fusion) | copy-start | bytes 98308
  552.8 44.6 %copy-start.5 = (pred[8192]{0:T(1024)(128)(4,1)S(1)}, pred[8192]{0:T(1024)(128)(4,1)}, u32[]{:S(2)}) copy-start(pred[8192]{0:T(1024)(128)(4,1)} %get-tuple-element.9) | copy-start | bytes 24580
  597.4 12.7 %copy-start.1 = (f32[768,32]{0,1:T(8,128)S(1)}, f32[768,32]{0,1:T(8,128)}, u32[]{:S(2)}) copy-start(f32[768,32]{0,1:T(8,128)} %param.7) | copy-start | bytes 294916

commit v2 on v1

v2 whole, which is shorter than its diff:
```python
import jax
import jax.numpy as jnp
from jax import lax
from jax.experimental import pallas as pl
from jax.experimental.pallas import tpu as pltpu
from jax.sharding import PartitionSpec as P

AXES = ("dp", "ep")
MESH = pl.DeviceIdType.MESH
PAIRS = 4


def exchange_body(disp, w_in, w_out, wb_in, wc_in,
                  back, wb_out, wc_out, wd_in, wd_out, relay,
                  xs, wi, wo, hid, x_send, x_recv, w_send, w_recv, r_send, b_recv, w_load, relay_recv, relay_send):
    x = lax.axis_index("dp")
    ep = lax.axis_index("ep")
    z, y, c = ep // 4, (ep // 2) % 2, ep % 2
    inner = (z == 1) | (z == 2)
    outer = jnp.logical_not(inner)
    z_near = z + 1 - 2 * (z % 2)
    z_mid = 3 - z
    cap, dim = xs.shape[2:]
    hidden = wi.shape[2]
    tiles, tile_out = wo.shape[1], wo.shape[3]
    rows = 2 * cap
    tile_in = 512

    def device(m, slab):
        return ((x + m // 4) % 2, slab * 4 + ((y + (m // 2) % 2) % 2) * 2 + (c + m % 2) % 2)

    def remote(src, dst, send, recv, dev):
        return pltpu.make_async_remote_copy(src, dst, send, recv, device_id=dev, device_id_type=MESH)

    barrier = pltpu.get_barrier_semaphore()
    for m in range(1, 8):
        pl.semaphore_signal(barrier, inc=1, device_id=device(m, z), device_id_type=MESH)
    for m in range(8):
        pl.semaphore_signal(barrier, inc=1, device_id=device(m, z_near), device_id_type=MESH)
    pl.semaphore_signal(barrier, inc=1, device_id=device(0, z_mid), device_id_type=MESH)
    pl.semaphore_wait(barrier, 16)

    def cols(t):
        return pl.ds(t * tile_out, tile_out)

    def weight(src, dst, k, slab):
        return remote(src, dst, w_send.at[k], w_recv.at[k], device(0, slab))

    send_b = [weight(w_out.at[x, :, cols(t)], wb_out.at[t], t, z_near) for t in range(tiles)]
    send_c = [weight(w_out.at[x, :, cols(t)], wc_out.at[t], 3 + t, z_mid) for t in range(tiles)]
    send_di = weight(wb_in, wd_in, 6, z_mid)
    send_do = [weight(wb_out.at[t], wd_out.at[t], 7 + t, z_mid) for t in range(tiles)]

    def load(src, dst, k):
        return pltpu.make_async_copy(src, dst, w_load.at[k])

    load_a = [load(w_in.at[x], wi.at[0], 0)] + [load(w_out.at[x, :, cols(t)], wo.at[0, t], 1 + t) for t in range(tiles)]
    load_b = [load(wb_in, wi.at[0], 0), load(wb_out, wo.at[0], 1)]
    load_c = [load(wc_in, wi.at[1], 4), load(wc_out, wo.at[1], 5)]
    load_di = load(wd_in, wi.at[1], 4)
    load_do = [load(wd_out.at[t], wo.at[1, t], 5 + t) for t in range(tiles)]

    def landed(sem):
        pltpu.make_async_copy(xs.at[0, 0], xs.at[0, 0], sem).wait()

    def own(q, r):
        return pltpu.make_async_copy(disp.at[q, 0], xs.at[r, 0], x_recv.at[r, 0])

    def dispatch(q, r, m, slab):
        return remote(disp.at[q, m], xs.at[r, m], x_send.at[q, m], x_recv.at[r, m], device(m, slab))

    @pl.when(inner)
    def _():
        for copy in send_b + send_c + [send_di]:
            copy.start()

    def hand(k, m):
        return remote(disp.at[2 + k, m], relay.at[k, m], x_send.at[2 + k, m], relay_recv.at[k, m], device(m, z))

    def forward(k, m):
        src = relay.at[k, m] if m else disp.at[2 + k, 0]
        return remote(src, xs.at[2 + 2 * k, m], relay_send.at[k, m], x_recv.at[2 + 2 * k, m], device(0, z_near))

    order = (1, 2, 4, 3, 5, 6, 7)

    @pl.when(outer)
    def _():
        for m in order:
            hand(0, m).start()
        forward(0, 0).start()
        send_b[0].start()

    own(0, 0).start()
    own(1, 3).start()
    for copy in load_a:
        copy.start()

    for m in order:
        dispatch(0, 0, m, z).start()

    @pl.when(inner)
    def _():
        load_c[0].start()
        own(2, 1).start()
        own(3, 5).start()
        for m in order:
            dispatch(2, 1, m, z).start()

    @pl.when(outer)
    def _():
        for m in order:
            hand(1, m).start()

    for m in order:
        dispatch(1, 3, m, z).start()

    @pl.when(inner)
    def _():
        for m in order:
            dispatch(3, 5, m, z).start()

    def pass_on(k, m):
        landed(relay_recv.at[k, m])
        forward(k, m).start()

    @pl.when(outer)
    def _():
        for m in order:
            pass_on(0, m)
        send_b[1].start()
        send_b[2].start()

    def first(r, p, b, kept):
        view = xs.at[r]

        def step(n, carry):
            span = pl.ds(pl.multiple_of(n * tile_in, tile_in), tile_in)
            value = jnp.dot(view[pl.ds(2 * p, 2)].reshape(rows, dim), wi[b, :, span], preferred_element_type=jnp.float32)
            kept[:, span] = jnp.maximum(value, 0.0).astype(jnp.bfloat16)
            return carry

        lax.fori_loop(0, hidden // tile_in, step, 0)

    def second(r, p, b, kept, t):
        value = jnp.dot(kept[...], wo[b, t], preferred_element_type=jnp.float32)
        span = pl.ds(pl.multiple_of(t * tile_out, tile_out), tile_out)
        xs[r, pl.ds(2 * p, 2), :, span] = value.astype(jnp.bfloat16).reshape(2, cap, tile_out)

    def each(lo, hi, fn):
        def step(i, carry):
            fn(i)
            return carry

        lax.fori_loop(lo, hi, step, 0)

    def send_back(r, q, p, edge):
        slab = jnp.where(edge, z_near, z)

        def result(m):
            return remote(xs.at[r, m], back.at[q, m], r_send.at[r, m], b_recv.at[q, m], device(m, slab))

        keep = (p == 0) & jnp.logical_not(edge)

        @pl.when(keep)
        def _():
            pltpu.make_async_copy(xs.at[r, 0], back.at[q, 0], b_recv.at[q, 0]).start()

        @pl.when(jnp.logical_not(keep))
        def _():
            result(2 * p).start()

        result(2 * p + 1).start()

    def whole(r, q, p, b, edge):
        landed(x_recv.at[r, 2 * p])
        landed(x_recv.at[r, 2 * p + 1])
        first(r, p, b, hid.at[0])
        each(0, tiles, lambda t: second(r, p, b, hid.at[0], t))
        send_back(r, q, p, edge)

    def late_step(s):
        is_first = (s < 4) | (s == 8) | (s == 13)
        k = jnp.where(s < 2, 4 + s, jnp.where(s < 6, s % 2, jnp.where(s < 8, s - 2, jnp.where(s < 10, 2, jnp.where(s < 13, s - 10, jnp.where(s < 16, 3, jnp.where(s < 18, s - 12, s % 6)))))))
        t = jnp.where((s < 10) | (s == 14), 0, jnp.where(s < 18, 1, 2))
        edge = k < 4
        r = jnp.where(edge, 4, 5)
        p = jnp.where(edge, k, 7 - k)
        slab = jnp.where(edge, z_near, z)
        spare = wi.at[0, pl.ds(0, rows)]

        for step, tile in ((4, 0), (10, 1), (18, 2)):
            @pl.when(s == step)
            def _():
                send_do[tile].wait_recv()
                load_do[tile].start()
                load_do[tile].wait()

        @pl.when(is_first)
        def _():
            landed(x_recv.at[r, 2 * p])
            landed(x_recv.at[r, 2 * p + 1])

            @pl.when(k < 5)
            def _():
                first(r, p, 1, hid.at[k])

            @pl.when(k == 5)
            def _():
                first(r, p, 1, spare)

        @pl.when(jnp.logical_not(is_first))
        def _():
            @pl.when(k < 5)
            def _():
                second(r, p, 1, hid.at[k], t)

            @pl.when(k == 5)
            def _():
                second(r, p, 1, spare, t)

            for i in range(2):
                m = 2 * p + i
                span = pl.ds(pl.multiple_of(t * tile_out, tile_out), tile_out)
                remote(xs.at[r, m, :, span], back.at[3, m, :, span], r_send.at[r, m], b_recv.at[3, m], device(m, slab)).start()

    def job(j, carry):
        g = jnp.where(inner, j // PAIRS, 3 * (j // PAIRS))
        start = j % PAIRS == 0
        p = jnp.where(g == 4, 1 - j % PAIRS, j % PAIRS)

        @pl.when((g == 0) & start)
        def _():
            for copy in load_a:
                copy.wait()

        @pl.when((g == 1) & start)
        def _():
            for copy in send_c:
                copy.wait_recv()
            load_c[1].start()
            load_b[0].start()
            load_c[0].wait()
            load_c[1].wait()

        @pl.when((g == 3) & start)
        def _():
            @pl.when(inner)
            def _():
                for t in range(tiles):
                    send_b[t].wait_recv()
                    send_do[t].start()

            @pl.when(outer)
            def _():
                forward(1, 0).start()
                for m in order:
                    pass_on(1, m)
                for copy in send_b:
                    copy.wait_recv()
                load_b[0].start()

            load_b[1].start()
            load_b[0].wait()
            load_b[1].wait()

        @pl.when((g == 4) & start)
        def _():
            send_di.wait_recv()
            load_di.start()
            load_di.wait()
            each(0, 24, late_step)

        r = jnp.where(g == 4, 5, g)
        b = jnp.where((g == 0) | (g == 3), 0, 1)
        q = jnp.where(g == 0, 0, jnp.where(g == 3, 1, jnp.where(g == 4, 3, 2)))
        whole(r, q, p, b, g == 2)
        return carry

    lax.fori_loop(0, jnp.where(inner, 4 * PAIRS + 2, 2 * PAIRS), job, 0)

    for q in range(4):
        each(0, 8, lambda m: landed(b_recv.at[q, m]))
        each(1, 8, lambda m: landed(x_send.at[q, m]))
    for r in (0, 3):
        each(1, 8, lambda m: landed(r_send.at[r, m]))
    for copy in send_b:
        copy.wait_send()

    @pl.when(inner)
    def _():
        for r in (1, 2, 4, 5):
            each(0 if r in (2, 4) else 1, 8, lambda m: landed(r_send.at[r, m]))
        for copy in send_c + [send_di] + send_do:
            copy.wait_send()

    @pl.when(outer)
    def _():
        for k in range(2):
            each(0, 8, lambda m: landed(relay_send.at[k, m]))


def exchange(disp, w_in, w_out, wb_in, wc_in):
    _, _, cap, dim = disp.shape
    hidden = w_in.shape[2]
    anywhere = pl.BlockSpec(memory_space=pl.ANY)
    dma = pltpu.SemaphoreType.DMA
    bf16 = jnp.bfloat16
    tile = 256
    in_shape, out_shape = (dim, hidden), (dim // tile, hidden, tile)
    outs = [disp.shape, out_shape, out_shape, in_shape, out_shape, (2,) + disp.shape[1:]]
    return pl.pallas_call(
        exchange_body,
        in_specs=[anywhere] * 5,
        out_specs=[anywhere] * len(outs),
        out_shape=[jax.ShapeDtypeStruct(s, bf16) for s in outs],
        scratch_shapes=[
            pltpu.VMEM((6, 8, cap, dim), bf16),
            pltpu.VMEM((2,) + in_shape, bf16),
            pltpu.VMEM((2,) + out_shape, bf16),
            pltpu.VMEM((PAIRS + 1, 2 * cap, hidden), bf16),
            dma((4, 8)), dma((6, 8)), dma((10,)), dma((10,)), dma((6, 8)), dma((4, 8)), dma((8,)), dma((2, 8)), dma((2, 8)),
        ],
        compiler_params=pltpu.CompilerParams(collective_id=0, has_side_effects=True, vmem_limit_bytes=67043328),
        cost_estimate=pl.CostEstimate(flops=4 * 48 * cap * dim * hidden, bytes_accessed=100 << 20, transcendentals=0),
        name="exchange",
    )(disp, w_in, w_out, wb_in, wc_in)[0]


def lin(x, z, y, c):
    return x * 16 + z * 4 + y * 2 + c


DEVICES = [(x, z, y, c) for x in range(2) for z in range(4) for y in range(2) for c in range(2)]


def solution(mesh):
    swap_near = [(lin(x, z, y, c), lin(x, z ^ 1, y, c)) for x, z, y, c in DEVICES]
    swap_mid = [(lin(x, z, y, c), lin(x, 3 - z, y, c)) for x, z, y, c in DEVICES if z in (1, 2)]

    def local_block(tokens, expert_idx, w_router, w_in, w_out):
        tok_count, dim = tokens.shape
        num_experts = w_router.shape[1]
        capacity = (5 * tok_count + 4 * num_experts - 1) // (4 * num_experts)
        x = lax.axis_index("dp")
        ep = lax.axis_index("ep")
        z, y, c = ep // 4, (ep // 2) % 2, ep % 2

        wa_in = lax.dynamic_index_in_dim(w_in, x, 0, False)
        with jax.named_scope("weights_mid"):
            wc_in = lax.ppermute(wa_in, AXES, swap_mid)
        with jax.named_scope("weights_near"):
            wb_in = lax.ppermute(wa_in, AXES, swap_near)

        logits = jnp.dot(tokens.astype(jnp.float32), w_router, precision=lax.Precision.HIGHEST)
        router_prob = jax.nn.softmax(logits, axis=-1)
        chosen = expert_idx[:, None] == jnp.arange(num_experts, dtype=jnp.int32)[None, :]
        gate = jnp.sum(jnp.where(chosen, router_prob, 0.0), axis=-1)
        running = jnp.cumsum(chosen.astype(jnp.int32), axis=0) - 1
        position = jnp.sum(jnp.where(chosen, running, 0), axis=-1)

        bit_x, bit_c, bit_y, slab = expert_idx & 1, (expert_idx >> 1) & 1, (expert_idx >> 2) & 1, expert_idx >> 3
        mask = ((bit_x ^ x) << 2) | ((bit_y ^ y) << 1) | (bit_c ^ c)
        far = (slab >> 1) != (z >> 1)
        second = jnp.where(far, (slab == 0) | (slab == 3), slab != z)
        block = far.astype(jnp.int32) * 16 + second.astype(jnp.int32) * 8 + mask
        kept = position < capacity
        slot = jnp.where(kept, block * capacity + position, num_experts * capacity)
        holder = jnp.zeros((num_experts * capacity + 1,), jnp.int32).at[slot].set(jnp.arange(tok_count, dtype=jnp.int32))
        disp = jnp.take(tokens, holder[:-1], axis=0, mode="clip").reshape(4, 8, capacity, dim)

        back = exchange(disp, w_in, w_out, wb_in, wc_in)

        picked = jnp.take(back.reshape(num_experts * capacity, dim), jnp.where(kept, slot, 0), axis=0, mode="clip")
        scaled = (gate[:, None] * picked.astype(jnp.float32)).astype(jnp.bfloat16)
        return jnp.where(kept[:, None], scaled, jnp.zeros_like(scaled))

    return jax.shard_map(local_block, mesh=mesh, in_specs=(P(AXES, None), P(AXES), P(None, None), P("ep", None, None), P("ep", None, None)), out_specs=P(AXES, None), check_vma=False)
```

time: 614 us -> 544 us (0.89)
  Pallas kernels: 432 us -> 356 us
    pallas_call x1, Pallas kernels: 432 us -> 356 us  [exchange(): pl.pallas_call(exchange_body, in_specs=[anywhere] * 5, out_specs=[anywher...]
  transfers between devices with their start and end apart: 2 -> 2, of which waited for: 0 -> 0; matrix products, arithmetic and copies ran while one was open for 18% -> 21% of each run, Pallas kernels for 0% -> 0%
where the time goes in v2:
time: 544 us; the launch traced here: 536 us
  Pallas kernels  356 us (65%)
  local copies, waits for them, and re-layouts  135 us (25%)
  other arithmetic  26.2 us (5%)
  matrix products  13.8 us (3%)
    pallas_call x1, Pallas kernels, exchange(): pl.pallas_call(exchange_body, in_specs=[anywhere] * 5, out_specs=[anywher...  356 us
    gather x1, local copies, waits for them, and re-layouts, local_block(): jnp.take(tokens, holder[:-1], axis=0, mode='clip')  52.4 us
    gather x1, local copies, waits for them, and re-layouts, local_block(): jnp.take(back.reshape(num_experts * capacity, dim), jnp.where(kept, slot,...  46.6 us
    scatter x1, local copies, waits for them, and re-layouts, local_block(): jnp.zeros((num_experts * capacity + 1,), jnp.int32).at[slot]  30.5 us
    dot_general x1, matrix products, local_block(): jnp.dot(tokens.astype(jnp.float32), w_router, precision=lax.Precision.HIG...  13.8 us
    select_n x1, other arithmetic, local_block(): return jnp.where(kept[:, None], scaled, jnp.zeros_like(scaled))  12.7 us
  transfers between devices with their start and end apart: 2, of which 0 were waited for; matrix products, arithmetic and copies ran while one was open for 21% of the time, Pallas kernels for 0%

profile of v2, /device:TPU:13, one launch (start us, length us, event | category | flops | bytes accessed | tf_op | source)
XLA Modules:
  0.0 536.1 jit_solution(15244080291608423841)
XLA Ops:
  0.0 0.0 copy-start
  0.0 4.8 dynamic-slice_bitcast_fusion
  4.9 0.2 collective-permute-start
  5.0 4.3 collective-permute-start.1
  9.4 0.9 fusion.3
  10.3 9.5 %reduce-window.6 = s32[32,64,128]{2,1,0:T(8,128)S(1)} reduce-window(s32[32,64,128]{2,1,0:T(8,128)S(1)} %fusion.3, s32[]{:T(128)} %constant.66.clone.1), window={size=1x1x128 pad=0_0x0_0x127_0}, to_apply=%region_0.1 | reduce-window | flops 33292288 | bytes 2097156 | tf_op jit(solution)/shard_map/reduce-window
  19.8 0.9 slice_reduce_fusion
  20.7 0.2 reduce-window.9
  20.9 0.3 add_add_fusion
  21.3 0.0 copy-done
  21.3 0.8 fusion.2
  22.1 0.7 select_clamp_fusion
  22.7 30.5 %scatter_custom_fusion = s32[10241]{0:T(1024)S(1)} fusion(s32[8192]{0:T(1024)S(1)} %compare_select_fusion, s32[8192]{0:T(1024)S(1)} %iota.11, s32[]{:T(128)} %constant.66.clone.1), kind=kCustom, calls=%fused_computation.25 | custom fusion | bytes 40968 | tf_op jit(solution)/shard_map/scatter | solution.py:368
  53.2 0.0 copy-start.2
  53.2 52.4 %gather_fusion = bf16[10240,768]{1,0:T(8,128)(2,1)} fusion(bf16[8192,768]{1,0:T(8,128)(2,1)} %param.5, s32[10240]{0:T(1024)S(1)} %slice_clamp_fusion), kind=kCustom, calls=%fused_computation | custom fusion | bytes 31498240 | tf_op jit(solution)/shard_map/jit(_take)/gather | solution.py:369
  105.6 0.0 copy-done.2
  105.6 13.8 %fusion.8 = (f32[8192]{0:T(1024)S(1)}, f32[8192,32]{0,1:T(8,128)S(1)}) fusion(bf16[8192,768]{1,0:T(8,128)(2,1)} %param.5, f32[768,32]{0,1:T(8,128)S(1)} %copy-done.2), kind=kOutput, calls=%fused_computation.28 | convolution fusion | flops 2416173056 | bytes 13762560 | tf_op jit(solution)/shard_map/dot_general | solution.py:354
  119.4 0.2 fusion.4
  119.6 0.9 select_reduce_fusion
  120.5 0.0 collective-permute-done.wb_in
  120.5 0.0 collective-permute-done.1.wc_in
  120.5 356.4 %exchange.1 = (bf16[4,8,320,768]{3,2,1,0:T(8,128)(2,1)}, bf16[3,3072,256]{2,1,0:T(8,128)(2,1)}, bf16[3,3072,256]{2,1,0:T(8,128)(2,1)}, bf16[768,3072]{1,0:T(8,12...) custom-call(bf16[4,8,320,768]{3,2,1,0:T(8,128)(2,1)} %bitcast.22, bf16[2,768,3072]{2,1,0:T(8,128)(2,1)} %w_in.1, ...), custom_call_target="tpu_custom_call" | custom-call | flops 144955146240 | bytes 104857600 | tf_op jit(solution)/shard_map/exchange/pallas_call | solution.py:311
  476.9 0.0 copy-start.1
  476.9 0.0 copy-start.3
  476.9 46.6 %gather_fusion.1 = bf16[8192,768]{1,0:T(8,128)(2,1)} fusion(bf16[10240,768]{1,0:T(8,128)(2,1)} %bitcast.21, s32[8192]{0:T(1024)} %get-tuple-element.7), kind=kCustom, calls=%fused_computation.1 | custom fusion | bytes 25198592 | tf_op jit(solution)/shard_map/jit(_take)/gather | solution.py:373
  523.5 0.0 copy-done.1
  523.5 0.0 copy-done.3
  523.5 12.7 %fusion = bf16[8192,768]{1,0:T(8,128)(2,1)} fusion(bf16[8192,768]{1,0:T(8,128)(2,1)} %gather_fusion.1, f32[8192]{0:T(1024)S(1)} %copy-done.1, pred[8192]{0:T(1024)(128)(4,1)S(1)} %copy-done.3), kind=kLoop, calls=%fused_computation.4 | loop fusion | flops 25165824 | bytes 25206784 | tf_op jit(solution)/shard_map/jit(_where)/select_n | solution.py:375
  (3 shorter events, 0.0 us)
Async XLA Ops:
  0.0 21.3 %copy-start = (s32[8192]{0:T(1024)S(1)}, s32[8192]{0:T(1024)}, u32[]{:S(2)}) copy-start(s32[8192]{0:T(1024)} %param.6) | copy-start | bytes 98308
  4.9 115.6 %collective-permute-start = (bf16[768,3072]{1,0:T(8,128)(2,1)}, bf16[768,3072]{1,0:T(8,128)(2,1)}, u32[]{:S(2)}, u32[]{:S(2)}) collective-permute-start(bf16[768,3072]{1,0:T(8,128)(2,1)} %dynamic-slice_bitcast_fusion), channel_id=1, source_target_pairs={{0,4},{1,5},{2,6},{3,7},{4,0},{5,1},{6,2},{7,3},{8,12},{9,13},{10,... | collective-permute-start | bytes 14155784 | tf_op jit(solution)/shard_map/weights_near/ppermute | solution.py:352
  5.0 115.5 %collective-permute-start.1 = (bf16[768,3072]{1,0:T(8,128)(2,1)}, bf16[768,3072]{1,0:T(8,128)(2,1)}, u32[]{:S(2)}, u32[]{:S(2)}) collective-permute-start(bf16[768,3072]{1,0:T(8,128)(2,1)} %dynamic-slice_bitcast_fusion), channel_id=1, source_target_pairs={{4,8},{5,9},{6,10},{7,11},{8,4},{9,5},{10,6},{11,7},{20,24},{21,25... | collective-permute-start | bytes 14155784 | tf_op jit(solution)/shard_map/weights_mid/ppermute | solution.py:350
  53.2 52.4 %copy-start.2 = (f32[768,32]{0,1:T(8,128)S(1)}, f32[768,32]{0,1:T(8,128)}, u32[]{:S(2)}) copy-start(f32[768,32]{0,1:T(8,128)} %param.7) | copy-start | bytes 294916
  476.9 46.6 %copy-start.1 = (f32[8192]{0:T(1024)S(1)}, f32[8192]{0:T(1024)}, u32[]{:S(2)}) copy-start(f32[8192]{0:T(1024)} %select_reduce_fusion) | copy-start | bytes 98308
  476.9 46.6 %copy-start.3 = (pred[8192]{0:T(1024)(128)(4,1)S(1)}, pred[8192]{0:T(1024)(128)(4,1)}, u32[]{:S(2)}) copy-start(pred[8192]{0:T(1024)(128)(4,1)} %get-tuple-element.9) | copy-start | bytes 24580

commit v3 on v2

--- a/solution.py
+++ b/solution.py
@@ -10,9 +10,9 @@
 PAIRS = 4
 
 
-def exchange_body(disp, w_in, w_out, wb_in, wc_in,
+def exchange_body(disp, w_in, w_out, wb_in, wc_in, router,
                   back, wb_out, wc_out, wd_in, wd_out, relay,
-                  xs, wi, wo, hid, x_send, x_recv, w_send, w_recv, r_send, b_recv, w_load, relay_recv, relay_send):
+                  xs, wi, wo, hid, gates, nothing, x_send, x_recv, w_send, w_recv, r_send, b_recv, w_load, relay_recv, relay_send, zero_sem):
     x = lax.axis_index("dp")
     ep = lax.axis_index("ep")
     z, y, c = ep // 4, (ep // 2) % 2, ep % 2
@@ -63,6 +63,14 @@
     def landed(sem):
         pltpu.make_async_copy(xs.at[0, 0], xs.at[0, 0], sem).wait()
 
+    def home(q, m):
+        return back.at[q * 8 + m]
+
+    nothing[...] = jnp.zeros_like(nothing)
+    gates[...] = jnp.zeros_like(gates)
+    clear = pltpu.make_async_copy(nothing, back.at[32, pl.ds(0, nothing.shape[0])], zero_sem)
+    clear.start()
+
     def own(q, r):
         return pltpu.make_async_copy(disp.at[q, 0], xs.at[r, 0], x_recv.at[r, 0])
 
@@ -141,8 +149,24 @@
 
         lax.fori_loop(0, hidden // tile_in, step, 0)
 
-    def second(r, p, b, kept, t):
+    def gate(r, p, k):
+        part = xs[r, pl.ds(2 * p, 2)].reshape(rows, dim)
+        logits = jnp.dot(part, router[2], preferred_element_type=jnp.float32)
+        logits = logits + jnp.dot(part, router[1], preferred_element_type=jnp.float32)
+        logits = logits + jnp.dot(part, router[0], preferred_element_type=jnp.float32)
+        lane = lax.broadcasted_iota(jnp.int32, logits.shape, 1)
+        slab = jnp.where(r == 0, z, jnp.where(r == 3, z_near, jnp.where(r < 3, z_mid, 3 - z_near)))
+        expert = slab * 8 + y * 4 + c * 2 + x
+        logits = jnp.where(lane < 32, logits, -jnp.inf)
+        weight = jnp.exp(logits - jnp.max(logits, axis=1, keepdims=True))
+        chosen = jnp.sum(jnp.where(lane == expert, weight, 0.0), axis=1, keepdims=True)
+        gates[...] = jnp.where(lane == k, chosen / jnp.sum(weight, axis=1, keepdims=True), gates[...])
+
+    def second(r, p, b, kept, k, t):
         value = jnp.dot(kept[...], wo[b, t], preferred_element_type=jnp.float32)
+        lane = lax.broadcasted_iota(jnp.int32, gates.shape, 1)
+        scale = jnp.sum(jnp.where(lane == k, gates[...], 0.0), axis=1, keepdims=True)
+        value = scale * value.astype(jnp.bfloat16).astype(jnp.float32)
         span = pl.ds(pl.multiple_of(t * tile_out, tile_out), tile_out)
         xs[r, pl.ds(2 * p, 2), :, span] = value.astype(jnp.bfloat16).reshape(2, cap, tile_out)
 
@@ -157,13 +181,13 @@
         slab = jnp.where(edge, z_near, z)
 
         def result(m):
-            return remote(xs.at[r, m], back.at[q, m], r_send.at[r, m], b_recv.at[q, m], device(m, slab))
+            return remote(xs.at[r, m], home(q, m), r_send.at[r, m], b_recv.at[q, m], device(m, slab))
 
         keep = (p == 0) & jnp.logical_not(edge)
 
         @pl.when(keep)
         def _():
-            pltpu.make_async_copy(xs.at[r, 0], back.at[q, 0], b_recv.at[q, 0]).start()
+            pltpu.make_async_copy(xs.at[r, 0], home(q, 0), b_recv.at[q, 0]).start()
 
         @pl.when(jnp.logical_not(keep))
         def _():
@@ -174,8 +198,9 @@
     def whole(r, q, p, b, edge):
         landed(x_recv.at[r, 2 * p])
         landed(x_recv.at[r, 2 * p + 1])
+        gate(r, p, 0)
         first(r, p, b, hid.at[0])
-        each(0, tiles, lambda t: second(r, p, b, hid.at[0], t))
+        each(0, tiles, lambda t: second(r, p, b, hid.at[0], 0, t))
         send_back(r, q, p, edge)
 
     def late_step(s):
@@ -199,6 +224,7 @@
         def _():
             landed(x_recv.at[r, 2 * p])
             landed(x_recv.at[r, 2 * p + 1])
+            gate(r, p, k)
 
             @pl.when(k < 5)
             def _():
@@ -212,16 +238,16 @@
         def _():
             @pl.when(k < 5)
             def _():
-                second(r, p, 1, hid.at[k], t)
+                second(r, p, 1, hid.at[k], k, t)
 
             @pl.when(k == 5)
             def _():
-                second(r, p, 1, spare, t)
+                second(r, p, 1, spare, 5, t)
 
             for i in range(2):
                 m = 2 * p + i
                 span = pl.ds(pl.multiple_of(t * tile_out, tile_out), tile_out)
-                remote(xs.at[r, m, :, span], back.at[3, m, :, span], r_send.at[r, m], b_recv.at[3, m], device(m, slab)).start()
+                remote(xs.at[r, m, :, span], home(3, m).at[:, span], r_send.at[r, m], b_recv.at[3, m], device(m, slab)).start()
 
     def job(j, carry):
         g = jnp.where(inner, j // PAIRS, 3 * (j // PAIRS))
@@ -283,6 +309,7 @@
         each(1, 8, lambda m: landed(x_send.at[q, m]))
     for r in (0, 3):
         each(1, 8, lambda m: landed(r_send.at[r, m]))
+    clear.wait()
     for copy in send_b:
         copy.wait_send()
 
@@ -299,7 +326,7 @@
             each(0, 8, lambda m: landed(relay_send.at[k, m]))
 
 
-def exchange(disp, w_in, w_out, wb_in, wc_in):
+def exchange(disp, w_in, w_out, wb_in, wc_in, router):
     _, _, cap, dim = disp.shape
     hidden = w_in.shape[2]
     anywhere = pl.BlockSpec(memory_space=pl.ANY)
@@ -307,10 +334,10 @@
     bf16 = jnp.bfloat16
     tile = 256
     in_shape, out_shape = (dim, hidden), (dim // tile, hidden, tile)
-    outs = [disp.shape, out_shape, out_shape, in_shape, out_shape, (2,) + disp.shape[1:]]
+    outs = [(33, cap, dim), out_shape, out_shape, in_shape, out_shape, (2,) + disp.shape[1:]]
     return pl.pallas_call(
         exchange_body,
-        in_specs=[anywhere] * 5,
+        in_specs=[anywhere] * 5 + [pl.BlockSpec(memory_space=pltpu.VMEM)],
         out_specs=[anywhere] * len(outs),
         out_shape=[jax.ShapeDtypeStruct(s, bf16) for s in outs],
         scratch_shapes=[
@@ -318,12 +345,14 @@
             pltpu.VMEM((2,) + in_shape, bf16),
             pltpu.VMEM((2,) + out_shape, bf16),
             pltpu.VMEM((PAIRS + 1, 2 * cap, hidden), bf16),
-            dma((4, 8)), dma((6, 8)), dma((10,)), dma((10,)), dma((6, 8)), dma((4, 8)), dma((8,)), dma((2, 8)), dma((2, 8)),
+            pltpu.VMEM((2 * cap, 128), jnp.float32),
+            pltpu.VMEM((16, dim), bf16),
+            dma((4, 8)), dma((6, 8)), dma((10,)), dma((10,)), dma((6, 8)), dma((4, 8)), dma((8,)), dma((2, 8)), dma((2, 8)), dma,
         ],
         compiler_params=pltpu.CompilerParams(collective_id=0, has_side_effects=True, vmem_limit_bytes=67043328),
         cost_estimate=pl.CostEstimate(flops=4 * 48 * cap * dim * hidden, bytes_accessed=100 << 20, transcendentals=0),
         name="exchange",
-    )(disp, w_in, w_out, wb_in, wc_in)[0]
+    )(disp, w_in, w_out, wb_in, wc_in, router)[0]
 
 
 def lin(x, z, y, c):
@@ -351,10 +380,13 @@
         with jax.named_scope("weights_near"):
             wb_in = lax.ppermute(wa_in, AXES, swap_near)
 
-        logits = jnp.dot(tokens.astype(jnp.float32), w_router, precision=lax.Precision.HIGHEST)
-        router_prob = jax.nn.softmax(logits, axis=-1)
+        high = lax.reduce_precision(w_router, 8, 7)
+        middle = lax.reduce_precision(w_router - high, 8, 7)
+        low = (w_router - high) - middle
+        router = jnp.stack([high, middle, low]).astype(jnp.bfloat16)
+        router = jnp.pad(router, ((0, 0), (0, 0), (0, 128 - num_experts)))
+
         chosen = expert_idx[:, None] == jnp.arange(num_experts, dtype=jnp.int32)[None, :]
-        gate = jnp.sum(jnp.where(chosen, router_prob, 0.0), axis=-1)
         running = jnp.cumsum(chosen.astype(jnp.int32), axis=0) - 1
         position = jnp.sum(jnp.where(chosen, running, 0), axis=-1)
 
@@ -368,10 +400,8 @@
         holder = jnp.zeros((num_experts * capacity + 1,), jnp.int32).at[slot].set(jnp.arange(tok_count, dtype=jnp.int32))
         disp = jnp.take(tokens, holder[:-1], axis=0, mode="clip").reshape(4, 8, capacity, dim)
 
-        back = exchange(disp, w_in, w_out, wb_in, wc_in)
-
-        picked = jnp.take(back.reshape(num_experts * capacity, dim), jnp.where(kept, slot, 0), axis=0, mode="clip")
-        scaled = (gate[:, None] * picked.astype(jnp.float32)).astype(jnp.bfloat16)
-        return jnp.where(kept[:, None], scaled, jnp.zeros_like(scaled))
+        back = exchange(disp, w_in, w_out, wb_in, wc_in, router).reshape(-1, dim)
+
+        return jnp.take(back, slot, axis=0, mode="clip")
 
     return jax.shard_map(local_block, mesh=mesh, in_specs=(P(AXES, None), P(AXES), P(None, None), P("ep", None, None), P("ep", None, None)), out_specs=P(AXES, None), check_vma=False)

time: 544 us -> 519 us (0.954); the launches traced: 536 us -> 518 us
  matrix products: 13.8 us -> 0 us
  other arithmetic: 26.2 us -> 13.3 us
    dot_general x1 -> x0, matrix products: 13.8 us -> none  [local_block(): jnp.dot(tokens.astype(jnp.float32), w_router, precision=lax.Precision.HIG...]
    select_n x1 -> x0, other arithmetic: 12.7 us -> none  [local_block(): return jnp.where(kept[:, None], scaled, jnp.zeros_like(scaled))]
  transfers between devices with their start and end apart: 2 -> 2, of which waited for: 0 -> 2; matrix products, arithmetic and copies ran while one was open for 21% -> 19% of each run, Pallas kernels for 0% -> 0%
where the time goes in v3:
time: 519 us; the launch traced here: 518 us
  Pallas kernels  360 us (69%)
  local copies, waits for them, and re-layouts  137 us (26%)
  other arithmetic  13.3 us (3%)
    pallas_call x1, Pallas kernels, exchange(): pl.pallas_call(exchange_body, in_specs=[anywhere] * 5 + [pl.BlockSpec(mem...  360 us
    gather x1, local copies, waits for them, and re-layouts, local_block(): jnp.take(tokens, holder[:-1], axis=0, mode='clip')  52.3 us
    gather x1, local copies, waits for them, and re-layouts, local_block(): return jnp.take(back, slot, axis=0, mode='clip')  46.8 us
    scatter x1, local copies, waits for them, and re-layouts, local_block(): jnp.zeros((num_experts * capacity + 1,), jnp.int32).at[slot]  30.5 us
  transfers between devices with their start and end apart: 2, of which 2 were waited for; matrix products, arithmetic and copies ran while one was open for 19% of the time, Pallas kernels for 0%

profile of v3, /device:TPU:13, one launch (start us, length us, event | category | flops | bytes accessed | tf_op | source)
XLA Modules:
  0.0 517.7 jit_solution(15522881441355815635)
XLA Ops:
  0.0 0.0 copy-start
  0.0 4.8 dynamic-slice_bitcast_fusion
  4.9 3.2 collective-permute-start.1
  8.1 0.1 collective-permute-start
  8.2 0.9 fusion.5
  9.1 0.3 copy.10
  9.4 0.9 fusion.2
  10.3 9.5 %reduce-window.6 = s32[32,64,128]{2,1,0:T(8,128)S(1)} reduce-window(s32[32,64,128]{2,1,0:T(8,128)S(1)} %fusion.2, s32[]{:T(128)} %constant.63.clone.1), window={size=1x1x128 pad=0_0x0_0x127_0}, to_apply=%region_0.1 | reduce-window | flops 33292288 | bytes 2097156 | tf_op jit(solution)/shard_map/reduce-window
  19.9 0.9 slice_reduce_fusion
  20.8 0.2 reduce-window.9
  21.0 1.0 pad.4.router
  21.9 0.3 add_add_fusion
  22.3 0.0 copy-done
  22.3 0.8 fusion.1
  23.1 0.7 broadcast_clamp_fusion
  23.7 30.5 %scatter_custom_fusion = s32[10241]{0:T(1024)S(1)} fusion(s32[8192]{0:T(1024)S(1)} %compare_select_fusion, s32[8192]{0:T(1024)S(1)} %iota.11, s32[]{:T(128)} %constant.63.clone.1), kind=kCustom, calls=%fused_computation.28 | custom fusion | bytes 40968 | tf_op jit(solution)/shard_map/scatter | solution.py:400
  54.2 52.3 %gather_fusion = bf16[10240,768]{1,0:T(8,128)(2,1)} fusion(bf16[8192,768]{1,0:T(8,128)(2,1)} %param.5, s32[10240]{0:T(1024)S(1)} %slice_clamp_fusion), kind=kCustom, calls=%fused_computation | custom fusion | bytes 31498240 | tf_op jit(solution)/shard_map/jit(_take)/gather | solution.py:401
  106.6 3.0 collective-permute-done.1.wc_in
  109.5 1.1 collective-permute-done.wb_in
  110.6 360.3 %exchange.1 = (bf16[33,320,768]{2,1,0:T(8,128)(2,1)}, bf16[3,3072,256]{2,1,0:T(8,128)(2,1)}, bf16[3,3072,256]{2,1,0:T(8,128)(2,1)}, bf16[768,3072]{1,0:T(8,128)(...) custom-call(bf16[4,8,320,768]{3,2,1,0:T(8,128)(2,1)} %bitcast.27, bf16[2,768,3072]{2,1,0:T(8,128)(2,1)} %w_in.1, ...), custom_call_target="tpu_custom_call" | custom-call | flops 144955146240 | bytes 104857600 | tf_op jit(solution)/shard_map/exchange/pallas_call | solution.py:338
  470.9 46.8 %gather_fusion.1 = bf16[8192,768]{1,0:T(8,128)(2,1)} fusion(bf16[10560,768]{1,0:T(8,128)(2,1)} %bitcast.26, s32[8192]{0:T(1024)} %get-tuple-element.7), kind=kCustom, calls=%fused_computation.1 | custom fusion | bytes 25198592 | tf_op jit(solution)/shard_map/jit(_take)/gather | solution.py:405
  (4 shorter events, 0.0 us)
Async XLA Ops:
  0.0 22.3 %copy-start = (s32[8192]{0:T(1024)S(1)}, s32[8192]{0:T(1024)}, u32[]{:S(2)}) copy-start(s32[8192]{0:T(1024)} %param.6) | copy-start | bytes 98308
  4.9 104.7 %collective-permute-start.1 = (bf16[768,3072]{1,0:T(8,128)(2,1)}, bf16[768,3072]{1,0:T(8,128)(2,1)}, u32[]{:S(2)}, u32[]{:S(2)}) collective-permute-start(bf16[768,3072]{1,0:T(8,128)(2,1)} %dynamic-slice_bitcast_fusion), channel_id=1, source_target_pairs={{4,8},{5,9},{6,10},{7,11},{8,4},{9,5},{10,6},{11,7},{20,24},{21,25... | collective-permute-start | bytes 14155784 | tf_op jit(solution)/shard_map/weights_mid/ppermute | solution.py:379
  8.1 102.6 %collective-permute-start = (bf16[768,3072]{1,0:T(8,128)(2,1)}, bf16[768,3072]{1,0:T(8,128)(2,1)}, u32[]{:S(2)}, u32[]{:S(2)}) collective-permute-start(bf16[768,3072]{1,0:T(8,128)(2,1)} %dynamic-slice_bitcast_fusion), channel_id=1, source_target_pairs={{0,4},{1,5},{2,6},{3,7},{4,0},{5,1},{6,2},{7,3},{8,12},{9,13},{10,... | collective-permute-start | bytes 14155784 | tf_op jit(solution)/shard_map/weights_near/ppermute | solution.py:381

commit v4 on v3

--- a/solution.py
+++ b/solution.py
@@ -11,7 +11,7 @@
 
 
 def exchange_body(disp, w_in, w_out, wb_in, wc_in, router,
-                  back, wb_out, wc_out, wd_in, wd_out, relay,
+                  back, wb_out, wc_out, wd_in, wd_out, relay, wb_rest, wc_rest, wd_rest,
                   xs, wi, wo, hid, gates, nothing, x_send, x_recv, w_send, w_recv, r_send, b_recv, w_load, relay_recv, relay_send, zero_sem):
     x = lax.axis_index("dp")
     ep = lax.axis_index("ep")
@@ -43,6 +43,9 @@
     def cols(t):
         return pl.ds(t * tile_out, tile_out)
 
+    split = wb_in.shape[1]
+    most, rest = pl.ds(0, split), pl.ds(split, hidden - split)
+
     def weight(src, dst, k, slab):
         return remote(src, dst, w_send.at[k], w_recv.at[k], device(0, slab))
 
@@ -51,13 +54,18 @@
     send_di = weight(wb_in, wd_in, 6, z_mid)
     send_do = [weight(wb_out.at[t], wd_out.at[t], 7 + t, z_mid) for t in range(tiles)]
 
+    send_br = weight(w_in.at[x, :, rest], wb_rest, 10, z_near)
+    send_cr = weight(w_in.at[x, :, rest], wc_rest, 11, z_mid)
+    send_dr = weight(wb_rest, wd_rest, 12, z_mid)
+
     def load(src, dst, k):
         return pltpu.make_async_copy(src, dst, w_load.at[k])
 
     load_a = [load(w_in.at[x], wi.at[0], 0)] + [load(w_out.at[x, :, cols(t)], wo.at[0, t], 1 + t) for t in range(tiles)]
-    load_b = [load(wb_in, wi.at[0], 0), load(wb_out, wo.at[0], 1)]
-    load_c = [load(wc_in, wi.at[1], 4), load(wc_out, wo.at[1], 5)]
-    load_di = load(wd_in, wi.at[1], 4)
+    load_b = [load(wb_in, wi.at[0, :, most], 0), load(wb_out, wo.at[0], 1), load(wb_rest, wi.at[0, :, rest], 8)]
+    load_c = [load(wc_in, wi.at[1, :, most], 4), load(wc_out, wo.at[1], 5), load(wc_rest, wi.at[1, :, rest], 9)]
+    load_di = load(wd_in, wi.at[1, :, most], 4)
+    load_dr = load(wd_rest, wi.at[1, :, rest], 10)
     load_do = [load(wd_out.at[t], wo.at[1, t], 5 + t) for t in range(tiles)]
 
     def landed(sem):
@@ -79,7 +87,7 @@
 
     @pl.when(inner)
     def _():
-        for copy in send_b + send_c + [send_di]:
+        for copy in [send_br] + send_b + [send_cr] + send_c + [send_di]:
             copy.start()
 
     def hand(k, m):
@@ -135,6 +143,7 @@
     def _():
         for m in order:
             pass_on(0, m)
+        send_br.start()
         send_b[1].start()
         send_b[2].start()
 
@@ -162,13 +171,36 @@
         chosen = jnp.sum(jnp.where(lane == expert, weight, 0.0), axis=1, keepdims=True)
         gates[...] = jnp.where(lane == k, chosen / jnp.sum(weight, axis=1, keepdims=True), gates[...])
 
-    def second(r, p, b, kept, k, t):
-        value = jnp.dot(kept[...], wo[b, t], preferred_element_type=jnp.float32)
+    def finish(r, p, k, t, value):
         lane = lax.broadcasted_iota(jnp.int32, gates.shape, 1)
         scale = jnp.sum(jnp.where(lane == k, gates[...], 0.0), axis=1, keepdims=True)
         value = scale * value.astype(jnp.bfloat16).astype(jnp.float32)
         span = pl.ds(pl.multiple_of(t * tile_out, tile_out), tile_out)
         xs[r, pl.ds(2 * p, 2), :, span] = value.astype(jnp.bfloat16).reshape(2, cap, tile_out)
+
+    def second(r, p, b, kept, k, t):
+        finish(r, p, k, t, jnp.dot(kept[...], wo[b, t], preferred_element_type=jnp.float32))
+
+    blocks = hidden // dim
+
+    def first_split(r, p, region):
+        def step(i, carry):
+            span = pl.ds(pl.multiple_of(i * tile_out, tile_out), tile_out)
+            place = pl.ds(pl.multiple_of(i % tiles * tile_out, tile_out), tile_out)
+            value = jnp.dot(xs[r, pl.ds(2 * p, 2)].reshape(rows, dim), wi[1, :, span], preferred_element_type=jnp.float32)
+            value = jnp.maximum(value, 0.0).astype(jnp.bfloat16)
+            xs[region, pl.ds(2 * (i // tiles), 2), :, place] = value.reshape(2, cap, tile_out)
+            return carry
+
+        lax.fori_loop(0, hidden // tile_out, step, 0)
+
+    def second_split(r, p, region, k, t):
+        value = None
+        for n in range(blocks):
+            part = xs[region, pl.ds(2 * n, 2)].reshape(rows, dim)
+            term = jnp.dot(part, wo[1, t, pl.ds(n * dim, dim), :], preferred_element_type=jnp.float32)
+            value = term if value is None else value + term
+        finish(r, p, k, t, value)
 
     def each(lo, hi, fn):
         def step(i, carry):
@@ -204,16 +236,24 @@
         send_back(r, q, p, edge)
 
     def late_step(s):
-        is_first = (s < 4) | (s == 8) | (s == 13)
-        k = jnp.where(s < 2, 4 + s, jnp.where(s < 6, s % 2, jnp.where(s < 8, s - 2, jnp.where(s < 10, 2, jnp.where(s < 13, s - 10, jnp.where(s < 16, 3, jnp.where(s < 18, s - 12, s % 6)))))))
-        t = jnp.where((s < 10) | (s == 14), 0, jnp.where(s < 18, 1, 2))
+        is_first = (s < 2) | (s == 4) | (s == 5) | (s == 7) | (s == 11) | (s == 18) | (s == 19)
+        k = jnp.where(s == 4, 4, jnp.where(s == 7, 5, jnp.where(s < 4, s % 2, jnp.where(s < 7, 2, s - 8))))
+        k = jnp.where(s < 11, k, jnp.where(s < 14, 3, jnp.where(s < 18, 4 + s % 2, jnp.where(s < 24, 6 + s % 2, jnp.where(s < 28, 27 - s, s - 24)))))
+        early = (s < 8) | (s == 12) | (s == 14) | (s == 15) | (s == 20) | (s == 21)
+        t = jnp.where(early, 0, jnp.where(s < 24, 1, 2))
         edge = k < 4
         r = jnp.where(edge, 4, 5)
         p = jnp.where(edge, k, 7 - k)
         slab = jnp.where(edge, z_near, z)
         spare = wi.at[0, pl.ds(0, rows)]
 
-        for step, tile in ((4, 0), (10, 1), (18, 2)):
+        @pl.when(s == 18)
+        def _():
+            for q, region in ((0, 0), (2, 1)):
+                landed(b_recv.at[q, 0])
+                each(1, 8, lambda m: landed(r_send.at[region, m]))
+
+        for step, tile in ((2, 0), (8, 1), (24, 2)):
             @pl.when(s == step)
             def _():
                 send_do[tile].wait_recv()
@@ -234,6 +274,10 @@
             def _():
                 first(r, p, 1, spare)
 
+            @pl.when(k > 5)
+            def _():
+                first_split(r, p, k - 6)
+
         @pl.when(jnp.logical_not(is_first))
         def _():
             @pl.when(k < 5)
@@ -244,15 +288,29 @@
             def _():
                 second(r, p, 1, spare, 5, t)
 
-            for i in range(2):
-                m = 2 * p + i
-                span = pl.ds(pl.multiple_of(t * tile_out, tile_out), tile_out)
-                remote(xs.at[r, m, :, span], home(3, m).at[:, span], r_send.at[r, m], b_recv.at[3, m], device(m, slab)).start()
+            @pl.when(k > 5)
+            def _():
+                second_split(r, p, k - 6, k, t)
+
+            span = pl.ds(pl.multiple_of(t * tile_out, tile_out), tile_out)
+
+            def tile_back(m):
+                return remote(xs.at[r, m, :, span], home(3, m).at[:, span], r_send.at[r, m], b_recv.at[3, m], device(m, slab))
+
+            @pl.when(k == 7)
+            def _():
+                pltpu.make_async_copy(xs.at[5, 0, :, span], home(3, 0).at[:, span], b_recv.at[3, 0]).start()
+
+            @pl.when(k != 7)
+            def _():
+                tile_back(2 * p).start()
+
+            tile_back(2 * p + 1).start()
 
     def job(j, carry):
         g = jnp.where(inner, j // PAIRS, 3 * (j // PAIRS))
-        start = j % PAIRS == 0
-        p = jnp.where(g == 4, 1 - j % PAIRS, j % PAIRS)
+        p = j % PAIRS
+        start = p == 0
 
         @pl.when((g == 0) & start)
         def _():
@@ -261,17 +319,20 @@
 
         @pl.when((g == 1) & start)
         def _():
-            for copy in send_c:
+            for copy in [send_cr] + send_c:
                 copy.wait_recv()
             load_c[1].start()
+            load_c[2].start()
             load_b[0].start()
-            load_c[0].wait()
-            load_c[1].wait()
+            for copy in load_c:
+                copy.wait()
 
         @pl.when((g == 3) & start)
         def _():
             @pl.when(inner)
             def _():
+                send_br.wait_recv()
+                send_dr.start()
                 for t in range(tiles):
                     send_b[t].wait_recv()
                     send_do[t].start()
@@ -279,45 +340,50 @@
             @pl.when(outer)
             def _():
                 forward(1, 0).start()
-                for m in order:
+                for m in range(1, 8):
                     pass_on(1, m)
-                for copy in send_b:
+                for copy in [send_br] + send_b:
                     copy.wait_recv()
                 load_b[0].start()
 
             load_b[1].start()
-            load_b[0].wait()
-            load_b[1].wait()
-
-        @pl.when((g == 4) & start)
-        def _():
-            send_di.wait_recv()
-            load_di.start()
-            load_di.wait()
-            each(0, 24, late_step)
-
-        r = jnp.where(g == 4, 5, g)
+            load_b[2].start()
+            for copy in load_b:
+                copy.wait()
+
         b = jnp.where((g == 0) | (g == 3), 0, 1)
-        q = jnp.where(g == 0, 0, jnp.where(g == 3, 1, jnp.where(g == 4, 3, 2)))
-        whole(r, q, p, b, g == 2)
+        q = jnp.where(g == 0, 0, jnp.where(g == 3, 1, 2))
+        whole(g, q, p, b, g == 2)
         return carry
 
-    lax.fori_loop(0, jnp.where(inner, 4 * PAIRS + 2, 2 * PAIRS), job, 0)
+    lax.fori_loop(0, jnp.where(inner, 4 * PAIRS, 2 * PAIRS), job, 0)
+
+    @pl.when(inner)
+    def _():
+        send_di.wait_recv()
+        load_di.start()
+        send_dr.wait_recv()
+        load_dr.start()
+        load_di.wait()
+        load_dr.wait()
+        each(0, 32, late_step)
+
+    done = jnp.where(inner, 1, 0)
 
     for q in range(4):
-        each(0, 8, lambda m: landed(b_recv.at[q, m]))
+        each(done if q in (0, 2) else 0, 8, lambda m: landed(b_recv.at[q, m]))
         each(1, 8, lambda m: landed(x_send.at[q, m]))
-    for r in (0, 3):
-        each(1, 8, lambda m: landed(r_send.at[r, m]))
+    each(1, jnp.where(inner, 1, 8), lambda m: landed(r_send.at[0, m]))
+    each(1, 8, lambda m: landed(r_send.at[3, m]))
     clear.wait()
-    for copy in send_b:
+    for copy in [send_br] + send_b:
         copy.wait_send()
 
     @pl.when(inner)
     def _():
-        for r in (1, 2, 4, 5):
+        for r in (2, 4, 5):
             each(0 if r in (2, 4) else 1, 8, lambda m: landed(r_send.at[r, m]))
-        for copy in send_c + [send_di] + send_do:
+        for copy in [send_cr, send_dr] + send_c + [send_di] + send_do:
             copy.wait_send()
 
     @pl.when(outer)
@@ -334,7 +400,8 @@
     bf16 = jnp.bfloat16
     tile = 256
     in_shape, out_shape = (dim, hidden), (dim // tile, hidden, tile)
-    outs = [(33, cap, dim), out_shape, out_shape, in_shape, out_shape, (2,) + disp.shape[1:]]
+    rest = (dim, hidden - wb_in.shape[1])
+    outs = [(33, cap, dim), out_shape, out_shape, wb_in.shape, out_shape, (2,) + disp.shape[1:], rest, rest, rest]
     return pl.pallas_call(
         exchange_body,
         in_specs=[anywhere] * 5 + [pl.BlockSpec(memory_space=pltpu.VMEM)],
@@ -347,7 +414,7 @@
             pltpu.VMEM((PAIRS + 1, 2 * cap, hidden), bf16),
             pltpu.VMEM((2 * cap, 128), jnp.float32),
             pltpu.VMEM((16, dim), bf16),
-            dma((4, 8)), dma((6, 8)), dma((10,)), dma((10,)), dma((6, 8)), dma((4, 8)), dma((8,)), dma((2, 8)), dma((2, 8)), dma,
+            dma((4, 8)), dma((6, 8)), dma((13,)), dma((13,)), dma((6, 8)), dma((4, 8)), dma((11,)), dma((2, 8)), dma((2, 8)), dma,
         ],
         compiler_params=pltpu.CompilerParams(collective_id=0, has_side_effects=True, vmem_limit_bytes=67043328),
         cost_estimate=pl.CostEstimate(flops=4 * 48 * cap * dim * hidden, bytes_accessed=100 << 20, transcendentals=0),
@@ -374,13 +441,15 @@
         ep = lax.axis_index("ep")
         z, y, c = ep // 4, (ep // 2) % 2, ep % 2
 
-        wa_in = lax.dynamic_index_in_dim(w_in, x, 0, False)
+        early = w_in.shape[2] * 5 // 6
+        wa_in = lax.dynamic_slice(w_in, (x, 0, 0), (1, dim, early))[0]
         with jax.named_scope("weights_mid"):
             wc_in = lax.ppermute(wa_in, AXES, swap_mid)
         with jax.named_scope("weights_near"):
             wb_in = lax.ppermute(wa_in, AXES, swap_near)
 
-        high = lax.reduce_precision(w_router, 8, 7)
+        largest = float(jnp.finfo(jnp.bfloat16).max)
+        high = jnp.clip(lax.reduce_precision(w_router, 8, 7), -largest, largest)
         middle = lax.reduce_precision(w_router - high, 8, 7)
         low = (w_router - high) - middle
         router = jnp.stack([high, middle, low]).astype(jnp.bfloat16)
@@ -397,8 +466,13 @@
         block = far.astype(jnp.int32) * 16 + second.astype(jnp.int32) * 8 + mask
         kept = position < capacity
         slot = jnp.where(kept, block * capacity + position, num_experts * capacity)
-        holder = jnp.zeros((num_experts * capacity + 1,), jnp.int32).at[slot].set(jnp.arange(tok_count, dtype=jnp.int32))
-        disp = jnp.take(tokens, holder[:-1], axis=0, mode="clip").reshape(4, 8, capacity, dim)
+        row_of = block[:, None] == jnp.arange(num_experts, dtype=jnp.int32)[None, :]
+        at_position = position[:, None] == jnp.arange(capacity, dtype=jnp.int32)[None, :]
+        token = jnp.arange(tok_count, dtype=jnp.int32)
+        digits = [jnp.where(at_position, d[:, None], 0).astype(jnp.bfloat16) for d in (token // 128, token % 128)]
+        held = [jnp.einsum("te,tp->ep", row_of.astype(jnp.bfloat16), d, preferred_element_type=jnp.float32) for d in digits]
+        holder = (held[0] * 128.0 + held[1]).astype(jnp.int32).reshape(num_experts * capacity)
+        disp = jnp.take(tokens, holder, axis=0, mode="clip").reshape(4, 8, capacity, dim)
 
         back = exchange(disp, w_in, w_out, wb_in, wc_in, router).reshape(-1, dim)
 

time: 519 us -> 515 us (level); the launches traced: 518 us -> 506 us
  local copies, waits for them, and re-layouts: 137 us -> 106 us
  waiting for transfers between devices: 4.07 us -> 14.4 us
  Pallas kernels: 360 us -> 366 us
    scatter x1 -> x0, local copies, waits for them, and re-layouts: 30.5 us -> none  [local_block(): jnp.zeros((num_experts * capacity + 1,), jnp.int32).at[slot]]
    ppermute x1, waiting for transfers between devices: 2.97 us -> 13.3 us  [local_block(): wc_in = lax.ppermute(wa_in, AXES, swap_mid)]
    pallas_call x1, Pallas kernels: 360 us -> 366 us  [exchange(): pl.pallas_call(exchange_body, in_specs=[anywhere] * 5 + [pl.BlockSpec(mem...]
  transfers between devices with their start and end apart: 2 -> 2, of which waited for: 2 -> 2; matrix products, arithmetic and copies ran while one was open for 19% -> 14% of each run, Pallas kernels for 0% -> 0%
where the time goes in v4:
time: 515 us; the launch traced here: 506 us
  Pallas kernels  366 us (71%)
  local copies, waits for them, and re-layouts  106 us (21%)
  waiting for transfers between devices  14.4 us (3%)
  other arithmetic  13.3 us (3%)
    pallas_call x1, Pallas kernels, exchange(): pl.pallas_call(exchange_body, in_specs=[anywhere] * 5 + [pl.BlockSpec(mem...  366 us
    gather x1, local copies, waits for them, and re-layouts, local_block(): jnp.take(tokens, holder, axis=0, mode='clip').reshape(4, 8, capacity, dim)  52.3 us
    gather x1, local copies, waits for them, and re-layouts, local_block(): return jnp.take(back, slot, axis=0, mode='clip')  46.8 us
    ppermute x1, waiting for transfers between devices, local_block(): wc_in = lax.ppermute(wa_in, AXES, swap_mid)  13.3 us
  transfers between devices with their start and end apart: 2, of which 2 were waited for; matrix products, arithmetic and copies ran while one was open for 14% of the time, Pallas kernels for 0%

profile of v4, /device:TPU:13, one launch (start us, length us, event | category | flops | bytes accessed | tf_op | source)
XLA Modules:
  0.0 505.8 jit_solution(12940512393974416304)
XLA Ops:
  0.0 0.0 copy-start
  0.0 4.3 dynamic-slice_bitcast_fusion
  4.3 3.2 collective-permute-start.1
  7.5 0.1 collective-permute-start
  7.6 0.9 fusion.23
  8.6 0.3 copy.12
  8.9 0.9 fusion.13
  9.8 9.5 %reduce-window.6 = s32[32,64,128]{2,1,0:T(8,128)S(1)} reduce-window(s32[32,64,128]{2,1,0:T(8,128)S(1)} %fusion.13, s32[]{:T(128)} %constant.88.clone.1), window={size=1x1x128 pad=0_0x0_0x127_0}, to_apply=%region_0.1 | reduce-window | flops 33292288 | bytes 2097156 | tf_op jit(solution)/shard_map/reduce-window
  19.3 0.9 slice_reduce_fusion
  20.2 0.2 reduce-window.9
  20.5 0.3 add_add_fusion
  20.8 0.0 copy-done
  20.8 0.8 fusion.12
  21.6 0.7 select_clamp_fusion
  22.3 1.6 fusion.10
  23.8 1.6 fusion.9
  25.4 0.1 reshape.55
  25.5 0.9 pad.4.router
  26.5 52.3 %gather_fusion = bf16[10240,768]{1,0:T(8,128)(2,1)} fusion(bf16[8192,768]{1,0:T(8,128)(2,1)} %param.5, s32[10240]{0:T(1024)S(1)} %broadcast_clamp_fusion), kind=kCustom, calls=%fused_computation | custom fusion | bytes 31498240 | tf_op jit(solution)/shard_map/jit(_take)/gather | solution.py:475
  78.8 13.3 %collective-permute-done.1.wc_in = bf16[768,2560]{1,0:T(8,128)(2,1)} collective-permute-done((bf16[768,2560]{1,0:T(8,128)(2,1)}, bf16[768,2560]{1,0:T(8,128)(2,1)}, u32[]{:S(2)}, u32[]{:S(2)}) %collective-permute-start.1) | collective-permute-done | bytes 3932192 | tf_op jit(solution)/shard_map/weights_mid/ppermute | solution.py:447
  92.1 1.1 collective-permute-done.wb_in
  93.2 365.8 %exchange.1 = (bf16[33,320,768]{2,1,0:T(8,128)(2,1)}, bf16[3,3072,256]{2,1,0:T(8,128)(2,1)}, bf16[3,3072,256]{2,1,0:T(8,128)(2,1)}, bf16[768,2560]{1,0:T(8,128)(...) custom-call(bf16[4,8,320,768]{3,2,1,0:T(8,128)(2,1)} %bitcast.26, ...), custom_call_target="tpu_custom_call" | custom-call | flops 144955146240 | bytes 104857600 | tf_op jit(solution)/shard_map/exchange/pallas_call | solution.py:405
  459.1 46.8 %gather_fusion.1 = bf16[8192,768]{1,0:T(8,128)(2,1)} fusion(bf16[10560,768]{1,0:T(8,128)(2,1)} %bitcast.25, s32[8192]{0:T(1024)} %get-tuple-element.7), kind=kCustom, calls=%fused_computation.1 | custom fusion | bytes 25198592 | tf_op jit(solution)/shard_map/jit(_take)/gather | solution.py:479
  (4 shorter events, 0.0 us)
Async XLA Ops:
  0.0 20.8 %copy-start = (s32[8192]{0:T(1024)S(1)}, s32[8192]{0:T(1024)}, u32[]{:S(2)}) copy-start(s32[8192]{0:T(1024)} %param.6) | copy-start | bytes 98308
  4.3 87.8 %collective-permute-start.1 = (bf16[768,2560]{1,0:T(8,128)(2,1)}, bf16[768,2560]{1,0:T(8,128)(2,1)}, u32[]{:S(2)}, u32[]{:S(2)}) collective-permute-start(bf16[768,2560]{1,0:T(8,128)(2,1)} %dynamic-slice_bitcast_fusion), channel_id=1, source_target_pairs={{4,8},{5,9},{6,10},{7,11},{8,4},{9,5},{10,6},{11,7},{20,24},{21,25... | collective-permute-start | bytes 11796488 | tf_op jit(solution)/shard_map/weights_mid/ppermute | solution.py:447
  7.5 85.7 %collective-permute-start = (bf16[768,2560]{1,0:T(8,128)(2,1)}, bf16[768,2560]{1,0:T(8,128)(2,1)}, u32[]{:S(2)}, u32[]{:S(2)}) collective-permute-start(bf16[768,2560]{1,0:T(8,128)(2,1)} %dynamic-slice_bitcast_fusion), channel_id=1, source_target_pairs={{0,4},{1,5},{2,6},{3,7},{4,0},{5,1},{6,2},{7,3},{8,12},{9,13},{10,... | collective-permute-start | bytes 11796488 | tf_op jit(solution)/shard_map/weights_near/ppermute | solution.py:449
